TPU v7x, 32 devices: a whole 2x2x4 slice. The times are simulated.
32 devices in a mesh: lat: 4 (over y, x), lon: 8 (over z, core).
Axes of the slice: x: 2, y: 2, z: 4, core: 2. Of those that a mesh axis runs over, the one named last changes fastest.
Arguments:
- forcing: float32 [256, 2048], P('lat', 'lon'), may hold values from -32 to 32
- depth_east: float32 [256, 2048], P('lat', 'lon'), may hold values from 0.25 to 4
- depth_north: float32 [256, 2048], P('lat', 'lon'), may hold values from 0.25 to 4
- surface_term: float32 [256, 2048], P('lat', 'lon'), may hold values from 0.02 to 0.5
- ocean_mask: int32 [256, 2048], P('lat', 'lon'), may hold values 0 or 1
- cost_weights: float32 [8, 256, 2048], P(None, 'lat', 'lon'), may hold values from -6 to 6
Outputs:
- forcing_adjoint: float32 [8, 256, 2048], P(None, 'lat', 'lon')
- east_gradient: float32 [8, 256, 2048], P(None, 'lat', 'lon')
- north_gradient: float32 [8, 256, 2048], P(None, 'lat', 'lon')
Inputs may be any that keep to these rules, and one draw needn't show every extreme that they name: `ocean_mask`: 1 marks an ocean cell, 0 a land cell.
All inputs are finite; a program needn't handle non-finite values. No bound on the sum of `ocean_mask` on one device may be relied on, other than what follows from the above.
Results may differ from a plain program's by a relative error of at most 0.00018.
Values sent between devices are 32-bit elements; how exact they have to be, the bound alone decides.
A program may use at most 64 MiB of HBM per device.

v0:
```python
import functools

import jax
import jax.numpy as jnp
from jax import lax
from jax.experimental import pallas as pl
from jax.experimental.pallas import tpu as pltpu
from jax.sharding import PartitionSpec as P

ITERS = 6
MESH = pl.DeviceIdType.MESH
HR = 16
HB = 8
HC = 13
HW = 6


def cost_of(mu, proj):
    def dot(a, b):
        acc = [None] * (len(a) + len(b) - 1)
        for i, x in enumerate(a):
            for j, y in enumerate(b):
                if a is b and j < i:
                    continue
                pr = x * y
                if a is b and j > i:
                    pr = pr + pr
                for m in (i + j, abs(i - j)):
                    acc[m] = pr if acc[m] is None else acc[m] + pr
        tot = acc[0] * mu[0]
        for m in range(1, len(acc)):
            tot = tot + acc[m] * mu[m]
        return 0.5 * tot

    def apply(p):
        q = list(p) + [None]
        for k, x in enumerate(p):
            if k == 0:
                q[1] = -x if q[1] is None else q[1] - x
            else:
                hx = 0.5 * x
                q[k + 1] = -hx if q[k + 1] is None else q[k + 1] - hx
                q[k - 1] = q[k - 1] - hx
        return q

    one = jnp.ones_like(mu[0])
    z, p, rz, cost = [one], [one], mu[0], None
    for step in range(ITERS):
        q = apply(p)
        alpha = rz / dot(p, q)
        term = p[0] * proj[0]
        for k in range(1, len(p)):
            term = term + p[k] * proj[k]
        cost = alpha * term if cost is None else cost + alpha * term
        if step < ITERS - 1:
            z = [z[k] - alpha * q[k] for k in range(len(z))] + [-alpha * q[-1]]
            rz_new = dot(z, z)
            beta = rz_new / rz
            p = [z[k] + beta * p[k] for k in range(len(p))] + [z[-1]]
            rz = rz_new
    return cost


def roll(x, shift, axis):
    return pltpu.roll(x, shift % x.shape[axis], axis)


def east(x):
    return roll(x, -1, 1)


def north(x):
    return roll(x, -1, 0)


def kernel(nlat, nlon, stages, f_hbm, de_hbm, dn_hbm, st_hbm, mk_hbm, w_hbm, wp, pack, geo, coef,
           f_ref, de_ref, dn_ref, st_ref, mk_ref, w_ref, lsem,
           send_w, send_e, recv_e, recv_w, row_n, row_s, mrow_n, mrow_s, wrow_n, wrow_s,
           sums, ssem, rsem, *reduce_refs):
    lat, lon = lax.axis_index("lat"), lax.axis_index("lon")
    costs, rows, cols = w_ref.shape
    loads = [pltpu.make_async_copy(src, dst, lsem.at[i]) for i, (src, dst) in enumerate(
        zip((f_hbm, de_hbm, dn_hbm, st_hbm, mk_hbm, w_hbm),
            (f_ref, de_ref, dn_ref, st_ref, mk_ref, w_ref)))]
    for c in loads:
        c.start()

    def peer(dlat, dlon):
        return (lax.rem(lat + dlat + nlat, nlat), lax.rem(lon + dlon + nlon, nlon))

    peers = {(a % nlat, b % nlon) for a in (-1, 0, 1) for b in (-1, 0, 1)}
    peers |= {o for stage in stages for o in stage}
    peers = sorted(peers - {(0, 0)})
    barrier = pltpu.get_barrier_semaphore()
    for a, b in peers:
        pl.semaphore_signal(barrier, inc=1, device_id=peer(a, b), device_id_type=MESH)

    for c in loads:
        c.wait()

    lane = lax.broadcasted_iota(jnp.int32, (rows, 128), 1)
    wide = [f_ref, de_ref, dn_ref, st_ref, mk_ref]
    for ref, at, first in ((send_w, slice(0, 128), True), (send_e, slice(cols - 128, cols), False)):
        buf = jnp.zeros((rows, 128), jnp.float32)
        pos = 0
        for i in range(5 + costs):
            width = HC if i < 5 else HW
            tile = (wide[i][:, at] if i < 5 else w_ref[i - 5, :, at]).astype(jnp.float32)
            tile = roll(tile, pos if first else pos + width, 1)
            buf = jnp.where((lane >= pos) & (lane < pos + width), tile, buf)
            pos += width
        ref[...] = buf
    pl.semaphore_wait(barrier, len(peers))

    copies = []

    def send(src, dst, dev):
        i = len(copies)
        c = pltpu.make_async_remote_copy(src_ref=src, dst_ref=dst, send_sem=ssem.at[i],
                                         recv_sem=rsem.at[i], device_id=dev, device_id_type=MESH)
        c.start()
        copies.append(c)

    lo, hi = pl.ds(0, HR), pl.ds(rows - HR, HR)
    for src, dst, d in ((send_w, recv_e, -1), (send_e, recv_w, 1)):
        send(src.at[lo], dst.at[pl.ds(rows, HR)], peer(-1, d))
        send(src.at[hi], dst.at[pl.ds(rows + HR, HR)], peer(1, d))
        send(src, dst.at[pl.ds(0, rows)], peer(0, d))
    for i in range(5):
        src = wide[i]
        send(src.at[lo], row_n.at[i] if i < 4 else mrow_n, peer(-1, 0))
        send(src.at[hi], row_s.at[i] if i < 4 else mrow_s, peer(1, 0))
    early = len(copies)
    send(w_ref.at[:, pl.ds(0, HB)], wrow_n, peer(-1, 0))
    send(w_ref.at[:, pl.ds(rows - HB, HB)], wrow_s, peer(1, 0))
    for c in copies[:early]:
        c.wait_recv()

    full = rows + 2 * HR
    lane = lax.broadcasted_iota(jnp.int32, (full, 128), 1)
    got_e, got_w = recv_e[...], recv_w[...]

    def side(pos, width):
        a = roll(got_e, -pos, 1)
        b = roll(got_w, 128 - width - pos, 1)
        return jnp.where(lane < width, a, jnp.where(lane >= 128 - width, b, 0.0))

    def padded(i):
        if i < 4:
            top, mid, low = row_n[i], wide[i][...], row_s[i]
        else:
            top, mid, low = (r[...].astype(jnp.float32) for r in (mrow_n, mk_ref, mrow_s))
        return jnp.concatenate([jnp.concatenate([mid, top, low], axis=0), side(HC * i, HC)], axis=1)

    ringc = cols + 128
    row_id = lax.broadcasted_iota(jnp.int32, (full, ringc), 0)
    keep_n = (lat < nlat - 1).astype(jnp.float32)
    keep_s = (lat > 0).astype(jnp.float32)
    edge = jnp.where(row_id < rows, 1.0, jnp.where(row_id < rows + HR, keep_n, keep_s))
    wet = padded(4) * edge
    ex = padded(1) * wet * east(wet)
    ey = padded(2) * wet * north(wet)
    base = wet * padded(3) + 1.0 - wet
    diag = base + ex + roll(ex, 1, 1) + ey + roll(ey, 1, 0)
    rs = lax.rsqrt(diag)
    rs = rs * (1.5 - 0.5 * diag * rs * rs)
    rs_e, rs_n = rs * east(rs), rs * north(rs)
    e2 = 2.0 * ex * rs_e
    n2 = 2.0 * ey * rs_n

    def twice(v, e2, n2):
        return e2 * east(v) + roll(e2 * v, 1, 1) + n2 * north(v) + roll(n2 * v, 1, 0)

    us = [rs * padded(0)]
    us.append(0.5 * twice(us[0], e2, n2))
    for k in range(1, ITERS):
        us.append(twice(us[k], e2, n2) - us[k - 1])

    inner = [u[:rows, :cols] for u in us]
    rs_in = rs[:rows, :cols]

    def put(at, field):
        line = jnp.sum(field, axis=0, keepdims=True)
        tot = line[:, :128]
        for c in range(128, cols, 128):
            tot = tot + line[:, c:c + 128]
        sums[at:at + 1, :] = tot

    sums[...] = jnp.zeros_like(sums)
    mom = ITERS * costs
    for k in range(ITERS):
        put(mom + 2 * k, inner[k] * inner[k])
        put(mom + 2 * k + 1, inner[k] * inner[k + 1])
    for n in range(costs):
        wn = w_ref[n] * rs_in
        for k in range(ITERS):
            put(k * costs + n, wn * inner[k])
    nsum = sums.shape[0]
    lane_s = lax.broadcasted_iota(jnp.int32, (nsum, 128), 1)
    row_s_id = lax.broadcasted_iota(jnp.int32, (nsum, 128), 0)
    by_row = jnp.sum(sums[...], axis=1, keepdims=True)
    mine = jnp.sum(jnp.where(lane_s == row_s_id, by_row, 0.0), axis=0, keepdims=True)
    reduce_copies = []

    def start(stage, value):
        mailbox, got, ss, rv = reduce_refs[4 * stage:4 * stage + 4]
        mailbox[...] = value
        group = []
        for i, (a, b) in enumerate(stages[stage]):
            c = pltpu.make_async_remote_copy(src_ref=mailbox, dst_ref=got.at[i], send_sem=ss.at[i],
                                             recv_sem=rv.at[i], device_id=peer(a, b),
                                             device_id_type=MESH)
            c.start()
            group.append(c)
        reduce_copies.extend(group)
        return group

    def finish(stage, group, value):
        for c in group:
            c.wait_recv()
        for i in range(len(group)):
            value = value + reduce_refs[4 * stage + 1][i]
        return value

    group = start(0, mine)

    for c in copies[early:]:
        c.wait_recv()

    def cut(x):
        return jnp.concatenate([x[:rows + HB], x[full - HB:]], axis=0)

    rs_b = cut(rs)
    for n in range(costs):
        block = jnp.concatenate([w_ref[n], wrow_n[n], wrow_s[n]], axis=0)
        tile = cut(side(5 * HC + HW * n, HW))
        wp[n] = rs_b * jnp.concatenate([block, tile], axis=1)
    for k in range(ITERS + 1):
        pack[k] = cut(us[k])
    pack[ITERS + 1], pack[ITERS + 2], pack[ITERS + 3] = cut(e2), cut(n2), rs_b
    wet_in = wet[:rows, :cols]
    me = wet_in * east(wet)[:rows, :cols]
    mn = wet_in * north(wet)[:rows, :cols]
    geo[0], geo[1] = me, mn
    geo[2] = 2.0 * me * rs_e[:rows, :cols]
    geo[3] = 2.0 * mn * rs_n[:rows, :cols]
    total = finish(0, group, mine)
    for stage in range(1, len(stages)):
        total = finish(stage, start(stage, total), total)

    tot8 = jnp.broadcast_to(total, (costs, 128))
    lane8 = lax.broadcasted_iota(jnp.int32, (costs, 128), 1)
    sub8 = lax.broadcasted_iota(jnp.int32, (costs, 128), 0)

    def pick(index):
        return jnp.broadcast_to(
            jnp.sum(jnp.where(lane8 == index, tot8, 0.0), axis=1, keepdims=True), (costs, 128))

    proj = [pick(k * costs + sub8) for k in range(ITERS)]
    raw = [pick(mom + m) for m in range(2 * ITERS)]
    mu = [raw[0], raw[1]]
    for k in range(1, ITERS):
        mu += [2.0 * raw[2 * k] - raw[0], 2.0 * raw[2 * k + 1] - raw[1]]
    cost, pull = jax.vjp(cost_of, mu, proj)
    mu_bar, x = pull(jnp.ones_like(cost))
    even = [2.0 * mu_bar[2 * k] for k in range(ITERS)]
    odd = [2.0 * mu_bar[2 * k + 1] for k in range(ITERS)]
    even[0] = mu_bar[0] - 0.5 * sum(even[1:])
    odd[0] = mu_bar[1] - 0.5 * sum(odd[1:])
    for k in range(ITERS):
        coef[3 * k], coef[3 * k + 1], coef[3 * k + 2] = x[k], 2.0 * even[k], odd[k]
    for c in copies + reduce_copies:
        c.wait_send()


def adjoint_kernel(wp, pack, geo, coef, fa_hbm, ge_hbm, gn_hbm,
                   u_in, u_east, u_north, quad, fa_ref, ge_ref, gn_ref,
                   osem):
    costs, rows, cols = fa_ref.shape
    ringc = wp.shape[2]
    def results(n):
        return [pltpu.make_async_copy(src.at[n], dst.at[n], osem.at[i, n])
                for i, (src, dst) in enumerate(((fa_ref, fa_hbm), (ge_ref, ge_hbm), (gn_ref, gn_hbm)))]

    for k in range(ITERS):
        u = pack[k] if k else 0.5 * pack[0]
        u_in[k] = u[:rows, :cols]
        u_east[k] = east(u)[:rows, :cols]
        u_north[k] = north(u)[:rows, :cols]
        quad[k] = pack[k] + pack[k - 2] if k > 1 else pack[k]
    quad[ITERS] = 0.5 * pack[ITERS] + pack[ITERS - 2]

    def one(n, carry):
        def c(i):
            return jnp.concatenate([coef[i, pl.ds(n, 1), :]] * (ringc // 128), axis=1)

        wn = wp[n]
        ub = [pack.at[k] for k in range(ITERS + 1)]
        e2b, n2b = pack[ITERS + 1], pack[ITERS + 2]
        nxt = c(3 * ITERS - 1) * ub[ITERS - 1][...]
        nxt2 = None
        dd = nxt * quad[ITERS]
        eb = nb = du = None
        for k in range(ITERS - 1, -1, -1):
            le, ln = east(nxt), north(nxt)
            s2 = e2b * le + roll(e2b * nxt, 1, 1) + n2b * ln + roll(n2b * nxt, 1, 0)
            if k == 0:
                s2 = 0.5 * s2
            lin = nxt[:rows, :cols]
            ea = lin * u_east[k] + le[:rows, :cols] * u_in[k]
            na = lin * u_north[k] + ln[:rows, :cols] * u_in[k]
            eb = ea if eb is None else eb + ea
            nb = na if nb is None else nb + na
            seed = c(3 * k + 1) * ub[k][...] + c(3 * k + 2) * ub[k + 1][...]
            if k > 0:
                seed = seed + c(3 * k - 1) * ub[k - 1][...]
            lam = c(3 * k) * wn + seed + s2
            if nxt2 is not None:
                lam = lam - nxt2
            dd = dd + lam * quad[k]
            du = seed * ub[k][...] if du is None else du + seed * ub[k][...]
            nxt, nxt2 = lam, nxt
        rs = pack[ITERS + 3]
        fa_ref[n] = rs[:rows, :cols] * nxt[:rows, :cols]
        db = -(rs * rs) * (dd - 0.5 * du)
        db_in = db[:rows, :cols]
        ge_ref[n] = geo[2] * eb + geo[0] * (db_in + east(db)[:rows, :cols])
        gn_ref[n] = geo[3] * nb + geo[1] * (db_in + north(db)[:rows, :cols])
        for r in results(n):
            r.start()
        return carry

    lax.fori_loop(0, costs, one, 0)
    for n in range(costs):
        for r in results(n):
            r.wait()


def solution(mesh):
    nlat, nlon = mesh.shape["lat"], mesh.shape["lon"]

    def body(forcing, depth_east, depth_north, surface_term, ocean_mask, cost_weights):
        costs, rows, cols = cost_weights.shape
        full, ringc = rows + 2 * HR, cols + 128
        f32 = jnp.float32
        dma = pltpu.SemaphoreType.DMA
        nsum = -(-(ITERS * costs + 2 * ITERS) // 8) * 8
        every = [(a, b) for a in range(nlat) for b in range(nlon) if a or b]
        stages = [every] if len(every) < 64 else [
            [(0, b) for b in range(1, nlon)], [(a, 0) for a in range(1, nlat)]]
        reduce_scratch = [
            ref for g in stages for ref in (
                pltpu.VMEM((1, 128), f32), pltpu.VMEM((len(g), 1, 128), f32),
                dma((len(g),)), dma((len(g),)))]
        bf = rows + 2 * HB
        shapes = ((costs, bf, ringc), (ITERS + 4, bf, ringc), (4, rows, cols), (3 * ITERS, costs, 128))
        hbm = pl.BlockSpec(memory_space=pltpu.HBM)
        vmem = pl.BlockSpec(memory_space=pltpu.VMEM)
        mids = pl.pallas_call(
            functools.partial(kernel, nlat, nlon, stages),
            out_shape=[pltpu.VMEM(x, f32) for x in shapes],
            in_specs=[hbm] * 6,
            out_specs=[vmem] * 4,
            scratch_shapes=[
                *[pltpu.VMEM((rows, cols), f32)] * 4,
                pltpu.VMEM((rows, cols), jnp.int32),
                pltpu.VMEM((costs, rows, cols), f32),
                dma((6,)),
                pltpu.VMEM((rows, 128), f32),
                pltpu.VMEM((rows, 128), f32),
                pltpu.VMEM((full, 128), f32),
                pltpu.VMEM((full, 128), f32),
                pltpu.VMEM((4, HR, cols), f32),
                pltpu.VMEM((4, HR, cols), f32),
                pltpu.VMEM((HR, cols), jnp.int32),
                pltpu.VMEM((HR, cols), jnp.int32),
                pltpu.VMEM((costs, HB, cols), f32),
                pltpu.VMEM((costs, HB, cols), f32),
                pltpu.VMEM((nsum, 128), f32),
                dma((18,)),
                dma((18,)),
                *reduce_scratch,
            ],
            compiler_params=pltpu.CompilerParams(
                collective_id=0, has_side_effects=True, vmem_limit_bytes=32 * 1024 * 1024
            ),
        )(*[pltpu.with_memory_space_constraint(x, pltpu.HBM) for x in (
            forcing, depth_east, depth_north, surface_term, ocean_mask, cost_weights)])
        out = (costs, rows, cols)
        return pl.pallas_call(
            adjoint_kernel,
            out_shape=[jax.ShapeDtypeStruct(out, f32)] * 3,
            in_specs=[vmem] * 4,
            out_specs=[hbm] * 3,
            scratch_shapes=[
                *[pltpu.VMEM((ITERS, rows, cols), f32)] * 3,
                pltpu.VMEM((ITERS + 1, bf, ringc), f32),
                *[pltpu.VMEM(out, f32)] * 3,
                dma((3, costs)),
            ],
            compiler_params=pltpu.CompilerParams(vmem_limit_bytes=32 * 1024 * 1024),
        )(*[pltpu.with_memory_space_constraint(x, pltpu.VMEM) for x in mids])

    grid = P("lat", "lon")
    field = P(None, "lat", "lon")
    return jax.shard_map(
        body,
        mesh=mesh,
        in_specs=(grid, grid, grid, grid, grid, field),
        out_specs=(field, field, field),
        check_vma=False,
    )
```

profile of v0, /device:TPU:0, one launch (start us, length us, event | category | flops | bytes accessed | tf_op | source)
XLA Modules:
  0.0 30.1 jit_solution(3609427163679165094)
XLA Ops:
  0.6 20.1 %shard_map.85 = (f32[8,80,384]{2,1,0:T(8,128)S(1)}, f32[10,80,384]{2,1,0:T(8,128)S(1)}, f32[4,64,256]{2,1,0:T(8,128)S(1)}, f32[18,8,128]{2,1,0:T(8,128)S(1)}) custom-call(f32[64,256]{1,0:T(8,128)} %f_hbm.1, f32[64,256]{1,0:T(8,128)} %de_hbm.1, f32[64,256]{1,0:T(8,128)} %dn_hbm.1, f32[64,256]{1,0:T(8,128)} %st_hbm.1, s32[64,256]{1,0:T(8,128)} %mk_hbm.1, ...), custom_call_target="tpu_custom_call" | custom-call | tf_op jit(solution)/shard_map/pallas_call | solution.py:359
  20.7 9.4 %shard_map.86 = (f32[8,64,256]{2,1,0:T(8,128)}, f32[8,64,256]{2,1,0:T(8,128)}, f32[8,64,256]{2,1,0:T(8,128)}) custom-call(f32[8,80,384]{2,1,0:T(8,128)S(1)} %get-tuple-element.7.wp, f32[10,80,384]{2,1,0:T(8,128)S(1)} %get-tuple-element.8.pack, f32[4,64,256]{2,1,0:T(8,128)S(1)} %get-tuple-element.9.geo, f32[18,8,128]{2,1,0:T(8,128)S(1)} %get-tuple-element.10.coef), custom_call_target="tpu_custom_call" | custom-call | tf_op jit(solution)/shard_map/pallas_call | solution.py:390
where the time goes:
time: 30.2 us; the launch traced here: 30.1 us
  Pallas kernels  29.4 us (97%)
  between operations  0.64 us (2%)
    pallas_call x1, Pallas kernels, body(): pl.pallas_call(functools.partial(kernel, nlat, nlon, stages), out_shape=[...  20.1 us
    pallas_call x1, Pallas kernels, body(): pl.pallas_call(adjoint_kernel, out_shape=[jax.ShapeDtypeStruct(out, f32)]...  9.39 us

commit v1 on v0

v1 whole, which is shorter than its diff:
```python
import functools

import jax
import jax.numpy as jnp
from jax import lax
from jax.experimental import pallas as pl
from jax.experimental.pallas import tpu as pltpu
from jax.sharding import PartitionSpec as P

ITERS = 6
MESH = pl.DeviceIdType.MESH
HR = 16
HB = 8
HS = 5
BLOCK = 8
HC = 13
HW = 6
GROUP = 16
DEG = 2 * ITERS
CS, CC = 0, ITERS
CX = CC + ITERS
CH = CX + DEG - 1
CM = CH + DEG
NCOEF = CM + DEG


def coefficients(mu, proj):
    def gram(a, b):
        return 0.5 * (mu[a + b] + mu[abs(a - b)])

    h = {}
    for a in range(ITERS):
        for b in range(a, ITERS):
            h[a, b] = gram(a, b) - 0.5 * (gram(a, b + 1) + gram(a, abs(b - 1)))
    g, p = list(mu[:ITERS]), list(proj)
    low, inv = {}, []
    for i in range(ITERS):
        inv.append(1.0 / h[i, i])
        for j in range(i + 1, ITERS):
            low[j, i] = h[i, j] * inv[i]
        for j in range(i + 1, ITERS):
            for k in range(j, ITERS):
                h[j, k] = h[j, k] - low[j, i] * h[i, k]
            g[j] = g[j] - low[j, i] * g[i]
            p[j] = p[j] - low[j, i] * p[i]
    c, d = [None] * ITERS, [None] * ITERS
    for i in range(ITERS - 1, -1, -1):
        c[i], d[i] = g[i] * inv[i], p[i] * inv[i]
        for j in range(i + 1, ITERS):
            c[i] = c[i] - low[j, i] * c[j]
            d[i] = d[i] - low[j, i] * d[j]
    zero = jnp.zeros_like(c[0])
    cc = c + [zero, zero]
    res = [1.0 - c[0] + 0.5 * c[1], c[0] + 0.5 * cc[2] - c[1]]
    for j in range(2, ITERS + 1):
        res.append(0.5 * (cc[j - 1] + cc[j + 1]) - cc[j])
    bar = [zero] * DEG
    for a in range(ITERS):
        half = 0.5 * d[a]
        for j in range(ITERS + 1):
            t = half * res[j]
            bar[a + j] = bar[a + j] + t
            bar[abs(a - j)] = bar[abs(a - j)] + t
    return c, bar


def roll(x, shift, axis):
    return pltpu.roll(x, shift % x.shape[axis], axis)


def east(x):
    return roll(x, -1, 1)


def north(x):
    return roll(x, -1, 0)


def total_of(terms):
    acc = None
    for t in terms:
        acc = t if acc is None else acc + t
    return acc


def kernel(nlat, nlon, stages, f_hbm, de_hbm, dn_hbm, st_hbm, mk_hbm, w_hbm,
           un, ue, xe, xn, ww, v, ve, geo, dia, coef, us_side, vs_side,
           fields, mk_ref, w_ref, lsem,
           send_w, send_e, recv_e, recv_w, row_n, row_s, mrow_n, mrow_s, wrow_n, wrow_s,
           wsend_w, wsend_e, wrecv_e, wrecv_w, up, unn, e2r, n2r, rsr, comb, ssem, rsem, *reduce_refs):
    lat, lon = lax.axis_index("lat"), lax.axis_index("lon")
    rows, costs, cols = w_ref.shape
    for i, src in enumerate((f_hbm, de_hbm, dn_hbm, st_hbm)):
        pltpu.make_async_copy(src, fields.at[i], lsem.at[0]).start()
    pltpu.make_async_copy(mk_hbm, mk_ref, lsem.at[1]).start()
    for n in range(costs):
        pltpu.make_async_copy(w_hbm.at[n], w_ref.at[:, n, :], lsem.at[2]).start()

    def loaded(i, ref):
        pltpu.make_async_copy(ref, ref, lsem.at[i]).wait()

    def peer(dlat, dlon):
        return (lax.rem(lat + dlat + nlat, nlat), lax.rem(lon + dlon + nlon, nlon))

    peers = {(a % nlat, b % nlon) for a in (-1, 0, 1) for b in (-1, 0, 1)}
    peers |= {o for stage in stages for o in stage}
    peers = sorted(peers - {(0, 0)})
    barrier = pltpu.get_barrier_semaphore()
    for a, b in peers:
        pl.semaphore_signal(barrier, inc=1, device_id=peer(a, b), device_id_type=MESH)

    loaded(0, fields)
    loaded(1, mk_ref)

    lane = lax.broadcasted_iota(jnp.int32, (rows, 128), 1)
    wide = [fields.at[i] for i in range(4)] + [mk_ref]
    for ref, at, first in ((send_w, slice(0, 128), True), (send_e, slice(cols - 128, cols), False)):
        buf = jnp.zeros((rows, 128), jnp.float32)
        for i in range(5):
            pos = HC * i
            tile = wide[i][:, at].astype(jnp.float32)
            tile = roll(tile, pos if first else pos + HC, 1)
            buf = jnp.where((lane >= pos) & (lane < pos + HC), tile, buf)
        ref[...] = buf
    pl.semaphore_wait(barrier, len(peers))

    waits = []

    def send(whole, parts):
        i = len(waits)
        for src, dst, dev in parts:
            pltpu.make_async_remote_copy(src_ref=src, dst_ref=dst, send_sem=ssem.at[i], recv_sem=rsem.at[i],
                                         device_id=dev, device_id_type=MESH).start()
        waits.append(pltpu.make_async_remote_copy(src_ref=whole, dst_ref=whole, send_sem=ssem.at[i],
                                                  recv_sem=rsem.at[i], device_id=peer(0, 1), device_id_type=MESH))

    lo, hi = pl.ds(0, HR), pl.ds(rows - HR, HR)
    send(row_n, [(fields.at[:, lo], row_n, peer(-1, 0))])
    send(row_s, [(fields.at[:, hi], row_s, peer(1, 0))])
    send(mrow_n, [(mk_ref.at[lo], mrow_n, peer(-1, 0))])
    send(mrow_s, [(mk_ref.at[hi], mrow_s, peer(1, 0))])
    for src, dst, d in ((send_w, recv_e, -1), (send_e, recv_w, 1)):
        send(dst, [(src.at[lo], dst.at[pl.ds(rows, HR)], peer(-1, d)),
                   (src.at[hi], dst.at[pl.ds(rows + HR, HR)], peer(1, d)),
                   (src, dst.at[pl.ds(0, rows)], peer(0, d))])
    early = len(waits)
    loaded(2, w_ref)
    send(wrow_n, [(w_ref.at[pl.ds(0, HW)], wrow_n, peer(-1, 0))])
    send(wrow_s, [(w_ref.at[pl.ds(rows - HS, HS)], wrow_s, peer(1, 0))])
    lane8 = lax.broadcasted_iota(jnp.int32, (costs, 128), 1)
    sub8 = lax.broadcasted_iota(jnp.int32, (costs, 128), 0)
    for j in range(rows // 8):
        to_w, to_e = jnp.zeros((costs, 128), jnp.float32), jnp.zeros((costs, 128), jnp.float32)
        for g in range(8):
            at = GROUP * g
            first, last = w_ref[8 * j + g, :, :128], w_ref[8 * j + g, :, cols - 128:]
            to_w = jnp.where((lane8 >= at) & (lane8 < at + HW), roll(first, at, 1), to_w)
            end = at if g else 128
            to_e = jnp.where((lane8 >= end - HS) & (lane8 < end), roll(last, at, 1), to_e)
        wsend_w[j], wsend_e[j] = to_w, to_e
    strips = rows // 8
    for src, dst, d in ((wsend_w, wrecv_e, -1), (wsend_e, wrecv_w, 1)):
        send(dst, [(src, dst.at[pl.ds(0, strips)], peer(0, d)),
                   (src.at[pl.ds(0, 1)], dst.at[pl.ds(strips, 1)], peer(-1, d)),
                   (src.at[pl.ds(strips - 1, 1)], dst.at[pl.ds(strips + 1, 1)], peer(1, d))])
    for c in waits[:early]:
        c.wait_recv()

    full = rows + 2 * HR
    lane = lax.broadcasted_iota(jnp.int32, (full, 128), 1)
    got_e, got_w = recv_e[...], recv_w[...]

    def side(pos, width):
        a = roll(got_e, -pos, 1)
        b = roll(got_w, 128 - width - pos, 1)
        return jnp.where(lane < width, a, jnp.where(lane >= 128 - width, b, 0.0))

    def padded(i):
        if i < 4:
            top, mid, low = row_n[i], wide[i][...], row_s[i]
        else:
            top, mid, low = (r[...].astype(jnp.float32) for r in (mrow_n, mk_ref, mrow_s))
        return jnp.concatenate([jnp.concatenate([mid, top, low], axis=0), side(HC * i, HC)], axis=1)

    ringc = cols + 128
    row_id = lax.broadcasted_iota(jnp.int32, (full, ringc), 0)
    keep_n = (lat < nlat - 1).astype(jnp.float32)
    keep_s = (lat > 0).astype(jnp.float32)
    edge = jnp.where(row_id < rows, 1.0, jnp.where(row_id < rows + HR, keep_n, keep_s))
    wet = padded(4) * edge
    ex = padded(1) * wet * east(wet)
    ey = padded(2) * wet * north(wet)
    base = wet * padded(3) + 1.0 - wet
    diag = base + ex + roll(ex, 1, 1) + ey + roll(ey, 1, 0)
    rs = lax.rsqrt(diag)
    rs = rs * (1.5 - 0.5 * diag * rs * rs)
    rs_e, rs_n = rs * east(rs), rs * north(rs)
    e2 = 2.0 * ex * rs_e
    n2 = 2.0 * ey * rs_n
    e2r[...], n2r[...], rsr[...] = e2, n2, rs
    rz = rows + HB

    lane_r = lax.broadcasted_iota(jnp.int32, (rows, 128), 1)
    row_r = lax.broadcasted_iota(jnp.int32, (rows, 128), 0)

    def to_lanes(column):
        return jnp.broadcast_to(jnp.sum(jnp.where(lane_r == row_r, column, 0.0), axis=0, keepdims=True), (costs, 128))

    def keep(k, u):
        un[k] = u[:rz, :cols]
        us_side[k] = to_lanes(u[:rows, cols:cols + 1])

    def step(k, x, prev, prev2, le, ln, e2, n2):
        s = e2 * le + roll(e2 * prev, 1, 1) + n2 * ln + roll(n2 * prev, 1, 0)
        return s if k == 1 else s - (prev2 + prev2 if k == 2 else prev2)

    us = [rs * padded(0)]
    for k in range(1, ITERS + 1):
        le, ln = east(us[k - 1]), north(us[k - 1])
        keep(k - 1, us[k - 1])
        ue[k - 1], unn[k - 1] = le[:rows, :cols], ln[:rows, :cols]
        us.append(step(k, None, us[k - 1], us[k - 2] if k > 1 else None, le, ln, e2, n2))
    keep(ITERS, us[ITERS])
    up[(ITERS - 1) % 2], up[ITERS % 2] = us[ITERS - 1], us[ITERS]

    inner = [u[:rows, :cols] for u in us]
    rs_in = rs[:rows, :cols]

    mom = ITERS * costs

    def fold(field):
        return total_of(field[i:i + 8, j:j + 128] for i in range(0, rows, 8) for j in range(0, cols, 128))

    mine = jnp.zeros((costs, 128), jnp.float32)
    for k in range(ITERS):
        for m, field in ((2 * k, inner[k] * inner[k]), (2 * k + 1, inner[k] * inner[k + 1])):
            mine = jnp.where(lane8 == mom + m, jnp.sum(fold(field), axis=1, keepdims=True), mine)
    proj = [None] * ITERS
    for r in range(rows):
        wr = w_ref[r] * rsr[r:r + 1, :cols]
        for k in range(ITERS):
            pr = wr * un[k, r:r + 1, :]
            proj[k] = pr if proj[k] is None else proj[k] + pr
    for k in range(ITERS):
        line = total_of(proj[k][:, j:j + 128] for j in range(0, cols, 128))
        mine = jnp.where(lane8 == costs * k + sub8, jnp.sum(line, axis=1, keepdims=True), mine)
    mine = jnp.sum(mine, axis=0, keepdims=True)

    def start(stage, value):
        mailbox, got, ss, rv = reduce_refs[4 * stage:4 * stage + 4]
        mailbox[...] = value
        for i, (a, b) in enumerate(stages[stage]):
            pltpu.make_async_remote_copy(src_ref=mailbox, dst_ref=got.at[i], send_sem=ss, recv_sem=rv,
                                         device_id=peer(a, b), device_id_type=MESH).start()
        all_of = pltpu.make_async_remote_copy(src_ref=got, dst_ref=got, send_sem=ss, recv_sem=rv,
                                              device_id=peer(0, 1), device_id_type=MESH)
        waits.append(all_of)
        return all_of

    def finish(stage, group, value):
        group.wait_recv()
        got = reduce_refs[4 * stage + 1]
        parts = [value] + [got[i] for i in range(len(stages[stage]))]
        while len(parts) > 1:
            parts = [sum(parts[i:i + 2][1:], parts[i]) for i in range(0, len(parts), 2)]
        return parts[0]

    first_reduce = len(waits)
    group = start(0, mine)

    for k in range(ITERS + 1, DEG):
        prev, prev2 = up[(k - 1) % 2], up[k % 2]
        le, ln = east(prev), north(prev)
        ue[k - 1], unn[k - 1] = le[:rows, :cols], ln[:rows, :cols]
        x = step(k, None, prev, prev2, le, ln, e2r[...], n2r[...])
        keep(k, x)
        up[k % 2] = x

    wet_in = wet[:rows, :cols]
    me = wet_in * east(wet)[:rows, :cols]
    mn = wet_in * north(wet)[:rows, :cols]
    geo[0], geo[1] = me, mn
    geo[2] = me * rs_e[:rows, :cols]
    geo[3] = mn * rs_n[:rows, :cols]
    geo[4] = rs_in
    rs_z = rsr[:rz, :cols]
    dia[...] = -0.5 * rs_z * rs_z
    rs_c = rsr[:rows, cols:cols + 1]
    us_side[DEG] = to_lanes(-0.5 * rs_c * rs_c)

    def products(t, carry):
        at = pl.ds(pl.multiple_of(t * 8, 8), 8)
        u = [un[k, at, :] for k in range(DEG)]
        for s in range(DEG):
            acc = None
            for a in range((s + 1) // 2):
                pr = u[a] * u[s - a]
                acc = pr if acc is None else acc + pr
            acc = acc + acc if acc is not None else None
            if s % 2 == 0:
                sq = u[s // 2] * u[s // 2]
                acc = sq if acc is None else acc + sq
            ww[s, at, :] = acc
        return carry

    def cross(t, carry):
        at = pl.ds(pl.multiple_of(t * 8, 8), 8)
        for src, dst in ((ue, xe), (unn, xn)):
            for s in range(DEG - 1):
                acc = None
                for a in range(s + 1):
                    pr = un[a, at, :cols] * src[s - a, at, :]
                    acc = pr if acc is None else acc + pr
                dst[s, at, :] = acc
        return carry

    lax.fori_loop(0, rz // 8, products, 0)
    lax.fori_loop(0, rows // 8, cross, 0)

    for c in waits[early:first_reduce]:
        c.wait_recv()

    for j in range(strips + 2):
        comb[j] = jnp.where(lane8 % GROUP < HW, wrecv_e[j], wrecv_w[j])

    def ring_row(r):
        return r if r >= 0 else full + r

    def line(ref, r):
        q = ring_row(r)
        return ref[q:q + 1, :]

    for r in range(-HS, rows + HW):
        if r < 0:
            block, packed, g = wrow_s[r + HS], comb[strips + 1], 8 + r
        elif r >= rows:
            block, packed, g = wrow_n[r - rows], comb[strips], r - rows
        else:
            block, packed, g = w_ref[r], comb[r // 8], r % 8
        side_r = roll(packed, -GROUP * g, 1)
        v[0, r + HS] = line(rsr, r) * jnp.concatenate([block, side_r], axis=1)

    for k in range(1, ITERS):
        for r in range(k - HS, rows + HW - k):
            x = v[k - 1, r + HS]
            e = line(e2r, r)
            le = east(x)
            y = e * le + roll(e * x, 1, 1) + line(n2r, r) * v[k - 1, r + HS + 1] + line(n2r, r - 1) * v[k - 1, r + HS - 1]
            if k > 1:
                before = v[k - 2, r + HS]
                y = y - (before + before if k == 2 else before)
            v[k, r + HS] = y
            if 0 <= r < rows:
                ve[k - 1, r] = le[:, :cols]
    for k in range(ITERS):
        acc = jnp.zeros((costs, 128), jnp.float32)
        for r in range(rows):
            acc = jnp.where(lane8 == r, roll(v[k, r + HS, :, cols:], r, 1), acc)
        vs_side[k] = acc

    total = finish(0, group, mine)
    for stage in range(1, len(stages)):
        total = finish(stage, start(stage, total), total)

    tot8 = jnp.broadcast_to(total, (costs, 128))
    def pick(index):
        return jnp.broadcast_to(
            jnp.sum(jnp.where(lane8 == index, tot8, 0.0), axis=1, keepdims=True), (costs, 128))

    proj = [pick(k * costs + sub8) * (0.5 if k else 1.0) for k in range(ITERS)]
    raw = [pick(mom + m) * (0.5 if m == 1 else 0.25 if m else 1.0) for m in range(DEG)]
    mu = [raw[0], raw[1]]
    for k in range(1, ITERS):
        mu += [2.0 * raw[2 * k] - raw[0], 2.0 * raw[2 * k + 1] - raw[1]]
    c, bar = coefficients(mu, proj)
    zero = jnp.zeros_like(c[0])
    acc = [zero] * (ITERS + 2)
    for m in range(ITERS - 1, -1, -1):
        acc[m] = c[m] + acc[m + 2]
    tail = [zero] * (DEG + 2)
    for m in range(DEG - 1, -1, -1):
        tail[m] = bar[m] + tail[m + 2]
    for m in range(ITERS):
        coef[CS + m] = acc[m]
        coef[CC + m] = 0.5 * c[m] if m else c[m]
    for s in range(DEG - 1):
        coef[CX + s] = 2.0 * tail[s + 1]
    for s in range(DEG):
        coef[CH + s] = tail[s] + tail[s + 2] if s else 2.0 * tail[0]
        coef[CM + s] = bar[s] if s else 2.0 * bar[0]
    for c in waits:
        c.wait_send()


def adjoint_kernel(un, ue, xe, xn, ww, v, ve, geo, dia, coef, us_side, vs_side,
                   fa_hbm, ge_hbm, gn_hbm, y, ye, z, fa_ref, ge_ref, gn_ref, osem):
    rows, costs, cols = fa_ref.shape
    rz = dia.shape[0]

    outs = ((fa_ref, fa_hbm), (ge_ref, ge_hbm), (gn_ref, gn_hbm))

    def factor(i, width, at=None):
        c = coef[i] if at is None else coef[i, at:at + 1]
        return jnp.concatenate([c] * (width // 128), axis=1)

    def vectors(u, width, at):
        return [total_of(factor(CS + a + b + 1, width, at) * u[b] for b in range(ITERS - 1 - a))
                for a in range(-1, ITERS - 1)]

    def diagonal(ys, u, width, at):
        out = [ys[0] + ys[2] + factor(CC, width, at) * u[0]]
        return out + [ys[a] + ys[a + 2] if a + 2 < len(ys) else ys[a] for a in range(1, ITERS)]

    def combine(t, carry):
        at = pl.ds(pl.multiple_of(t * 8, 8), 8)
        u = [un[k, at, :] for k in range(ITERS)]
        ys = vectors(u, cols, 0)
        for a, f in enumerate(diagonal(ys, u, cols, 0)):
            z[a, at, :] = f
        for a in range(ITERS - 1):
            y[a, at, :] = ys[a + 1]
        return carry

    def combine_east(t, carry):
        at = pl.ds(pl.multiple_of(t * 8, 8), 8)
        u = [ue[k, at, :] for k in range(ITERS - 1)]
        for a in range(ITERS - 1):
            ye[a, at, :] = total_of(factor(CS + a + b + 1, cols, 0) * u[b] for b in range(ITERS - 1 - a))
        return carry

    lax.fori_loop(0, rz // 8, combine, 0)
    lax.fori_loop(0, rows // 8, combine_east, 0)
    u = [us_side[k] for k in range(DEG)]
    zs = diagonal(vectors(u, 128, None), u, 128, None)
    side = total_of(zs[a] * vs_side[a] for a in range(ITERS))
    for s in range(DEG):
        side = side + coef[CH + s] * total_of(u[a] * u[s - a] for a in range(s + 1))
    side = side * us_side[DEG]
    lane_c = lax.broadcasted_iota(jnp.int32, (costs, cols), 1)

    def line(ref, *at):
        return ref[(*at[:-1], pl.ds(at[-1], 1), slice(None))]

    def diag_of(r):
        acc = total_of(line(z, a, r) * v[a, r + HS, :, :cols] for a in range(ITERS))
        for s in range(DEG):
            acc = acc + factor(CH + s, cols) * line(ww, s, r)
        return acc * line(dia, r)

    def row(r, above):
        ge = gn = fa = db = None

        def add(acc, term):
            return term if acc is None else acc + term

        for a in range(ITERS):
            x = v[a, r + HS, :, :cols]
            db = add(db, x * line(z, a, r))
            fa = add(fa, x * factor(CC + a, cols))
            if a < ITERS - 1:
                here = line(y, a, r)
                ge = add(ge, x * line(ye, a, r) + ve[a, r] * here)
                gn = add(gn, x * line(y, a, r + 1) + v[a, r + HS + 1, :, :cols] * here)
        for s in range(DEG):
            db = add(db, factor(CH + s, cols) * line(ww, s, r))
            fa = add(fa, factor(CM + s, cols) * line(un, s, r))
            if s < DEG - 1:
                c = factor(CX + s, cols)
                ge = add(ge, c * line(xe, s, r))
                gn = add(gn, c * line(xn, s, r))
        db = db * line(dia, r)
        end = jnp.concatenate([pltpu.roll(side, 127 - r, 1)] * (cols // 128), axis=1)
        db_e = jnp.where(lane_c == cols - 1, end, east(db))
        fa_ref[r] = line(geo, 4, r) * fa
        ge_ref[r] = line(geo, 2, r) * ge + line(geo, 0, r) * (db + db_e)
        gn_ref[r] = line(geo, 3, r) * gn + line(geo, 1, r) * (db + above)
        return db

    parts = 2
    size = rows // parts

    def block(i, above):
        first = rows - (i + 1) * BLOCK
        for j in range(BLOCK - 1, -1, -1):
            above = row(first + j, above)
        return above

    above = diag_of(rows)
    per = size // BLOCK
    for p in range(parts):
        above = lax.fori_loop(p * per, (p + 1) * per, block, above)
        at = pl.ds(rows - (p + 1) * size, size)
        for i, (src, dst) in enumerate(outs):
            for n in range(costs):
                pltpu.make_async_copy(src.at[at, n, :], dst.at[n, at], osem.at[i]).start()
    for i, (src, dst) in enumerate(outs):
        pltpu.make_async_copy(dst, dst, osem.at[i]).wait()


def solution(mesh):
    nlat, nlon = mesh.shape["lat"], mesh.shape["lon"]

    def body(forcing, depth_east, depth_north, surface_term, ocean_mask, cost_weights):
        costs, rows, cols = cost_weights.shape
        full, ringc = rows + 2 * HR, cols + 128
        f32 = jnp.float32
        dma = pltpu.SemaphoreType.DMA
        every = [(a, b) for a in range(nlat) for b in range(nlon) if a or b]
        stages = [every] if len(every) < 64 else [
            [(0, b) for b in range(1, nlon)], [(a, 0) for a in range(1, nlat)]]
        reduce_scratch = [
            ref for g in stages for ref in (
                pltpu.VMEM((1, 128), f32), pltpu.VMEM((len(g), 1, 128), f32),
                dma, dma)]
        rz = rows + HB
        shapes = (
            (DEG, rz, cols), (DEG - 1, rows, cols), (DEG - 1, rows, cols), (DEG - 1, rows, cols), (DEG, rz, cols),
            (ITERS, rows + HS + HW, costs, ringc), (ITERS - 1, rows, costs, cols),
            (5, rows, cols), (rz, cols), (NCOEF, costs, 128), (DEG + 1, costs, 128), (ITERS, costs, 128))
        hbm = pl.BlockSpec(memory_space=pltpu.HBM)
        vmem = pl.BlockSpec(memory_space=pltpu.VMEM)
        args = (forcing, depth_east, depth_north, surface_term, ocean_mask, cost_weights)
        mids = pl.pallas_call(
            functools.partial(kernel, nlat, nlon, stages),
            out_shape=[pltpu.VMEM(x, f32) for x in shapes],
            in_specs=[hbm] * 6,
            out_specs=[vmem] * len(shapes),
            scratch_shapes=[
                pltpu.VMEM((4, rows, cols), f32),
                pltpu.VMEM((rows, cols), jnp.int32),
                pltpu.VMEM((rows, costs, cols), f32),
                dma((3,)),
                pltpu.VMEM((rows, 128), f32),
                pltpu.VMEM((rows, 128), f32),
                pltpu.VMEM((full, 128), f32),
                pltpu.VMEM((full, 128), f32),
                pltpu.VMEM((4, HR, cols), f32),
                pltpu.VMEM((4, HR, cols), f32),
                pltpu.VMEM((HR, cols), jnp.int32),
                pltpu.VMEM((HR, cols), jnp.int32),
                pltpu.VMEM((HW, costs, cols), f32),
                pltpu.VMEM((HS, costs, cols), f32),
                *[pltpu.VMEM((rows // 8, costs, 128), f32)] * 2,
                *[pltpu.VMEM((rows // 8 + 2, costs, 128), f32)] * 2,
                pltpu.VMEM((2, full, ringc), f32),
                pltpu.VMEM((DEG - 1, rows, cols), f32),
                *[pltpu.VMEM((full, ringc), f32)] * 3,
                pltpu.VMEM((rows // 8 + 2, costs, 128), f32),
                dma((10,)),
                dma((10,)),
                *reduce_scratch,
            ],
            compiler_params=pltpu.CompilerParams(
                collective_id=0, has_side_effects=True, vmem_limit_bytes=24 * 1024 * 1024
            ),
        )(*[pltpu.with_memory_space_constraint(x, pltpu.HBM) for x in args])
        out = (costs, rows, cols)
        return pl.pallas_call(
            adjoint_kernel,
            out_shape=[jax.ShapeDtypeStruct(out, f32)] * 3,
            in_specs=[vmem] * len(shapes),
            out_specs=[hbm] * 3,
            scratch_shapes=[
                pltpu.VMEM((ITERS - 1, rz, cols), f32),
                pltpu.VMEM((ITERS - 1, rows, cols), f32),
                pltpu.VMEM((ITERS, rz, cols), f32),
                *[pltpu.VMEM((rows, costs, cols), f32)] * 3,
                dma((3,)),
            ],
            compiler_params=pltpu.CompilerParams(vmem_limit_bytes=24 * 1024 * 1024),
        )(*[pltpu.with_memory_space_constraint(x, pltpu.VMEM) for x in mids])

    grid = P("lat", "lon")
    field = P(None, "lat", "lon")
    return jax.shard_map(
        body,
        mesh=mesh,
        in_specs=(grid, grid, grid, grid, grid, field),
        out_specs=(field, field, field),
        check_vma=False,
    )
```

time: 30.2 us -> 25.4 us (0.84)
  Pallas kernels: 29.4 us -> 24.6 us
    pallas_call x1, Pallas kernels: 9.39 us -> 5.03 us  [body(): pl.pallas_call(adjoint_kernel, out_shape=[jax.ShapeDtypeStruct(out, f32)]...]
    pallas_call x1, Pallas kernels: 20.1 us -> 19.6 us  [body(): pl.pallas_call(functools.partial(kernel, nlat, nlon, stages), out_shape=[...]
where the time goes in v1:
time: 25.4 us; the launch traced here: 25.2 us
  Pallas kernels  24.6 us (97%)
  between operations  0.64 us (3%)
    pallas_call x1, Pallas kernels, body(): pl.pallas_call(functools.partial(kernel, nlat, nlon, stages), out_shape=[...  19.6 us
    pallas_call x1, Pallas kernels, body(): pl.pallas_call(adjoint_kernel, out_shape=[jax.ShapeDtypeStruct(out, f32)]...  5.03 us

profile of v1, /device:TPU:0, one launch (start us, length us, event | category | flops | bytes accessed | tf_op | source)
XLA Modules:
  0.0 25.2 jit_solution(1172122874767160212)
XLA Ops:
  0.6 19.6 %shard_map.85 = (f32[12,72,256]{2,1,0:T(8,128)S(1)}, f32[11,64,256]{2,1,0:T(8,128)S(1)}, f32[11,64,256]{2,1,0:T(8,128)S(1)}, f32[11,64,256]{2,1,0:T(8,128)S(1)},...) custom-call(f32[64,256]{1,0:T(8,128)} %f_hbm.1, ...), custom_call_target="tpu_custom_call" | custom-call | tf_op jit(solution)/shard_map/pallas_call | solution.py:523
  20.2 5.0 %shard_map.86 = (f32[8,64,256]{2,1,0:T(8,128)}, f32[8,64,256]{2,1,0:T(8,128)}, f32[8,64,256]{2,1,0:T(8,128)}) custom-call(f32[12,72,256]{2,1,0:T(8,128)S(1)} %get-tuple-element.15.un, f32[11,64,256]{2,1,0:T(8,128)S(1)} %get-tuple-element.16.ue, f32[11,64,256]{2,1,0:T(8,128)S(1)} %get-tuple-element.17.xe, f32[11,64,256]{2,1,0:T(8,128)S(1)} %get-tuple-element.18.xn, ...), custom_call_target="tpu_custom_call" | custom-call | tf_op jit(solution)/shard_map/pallas_call | solution.py:558

commit v2 on v1

--- a/solution.py
+++ b/solution.py
@@ -9,7 +9,6 @@
 
 ITERS = 6
 MESH = pl.DeviceIdType.MESH
-HR = 16
 HB = 8
 HS = 5
 BLOCK = 8
@@ -86,8 +85,10 @@
 def kernel(nlat, nlon, stages, f_hbm, de_hbm, dn_hbm, st_hbm, mk_hbm, w_hbm,
            un, ue, xe, xn, ww, v, ve, geo, dia, coef, us_side, vs_side,
            fields, mk_ref, w_ref, lsem,
-           send_w, send_e, recv_e, recv_w, row_n, row_s, mrow_n, mrow_s, wrow_n, wrow_s,
-           wsend_w, wsend_e, wrecv_e, wrecv_w, up, unn, e2r, n2r, rsr, comb, ssem, rsem, *reduce_refs):
+           send_w, send_e, recv_e, recv_w, far_e, far_w, row_n, row_s, far_n, far_s,
+           mrow_n, mrow_s, mfar_n, mfar_s, wrow_n, wrow_s,
+           wsend_w, wsend_e, wrecv_e, wrecv_w, up, unn, e2r, n2r, rsr, e2w, n2w, comb, ssem, rsem, hello,
+           *reduce_refs):
     lat, lon = lax.axis_index("lat"), lax.axis_index("lon")
     rows, costs, cols = w_ref.shape
     for i, src in enumerate((f_hbm, de_hbm, dn_hbm, st_hbm)):
@@ -102,12 +103,22 @@
     def peer(dlat, dlon):
         return (lax.rem(lat + dlat + nlat, nlat), lax.rem(lon + dlon + nlon, nlon))
 
-    peers = {(a % nlat, b % nlon) for a in (-1, 0, 1) for b in (-1, 0, 1)}
-    peers |= {o for stage in stages for o in stage}
-    peers = sorted(peers - {(0, 0)})
+    def ring(radius, lat_too, lon_too):
+        offs = {(a % nlat, b % nlon) for a in ((-radius, 0, radius) if lat_too else (0,))
+                for b in ((-radius, 0, radius) if lon_too else (0,))}
+        return sorted(offs - {(0, 0)})
+
+    def greet(sem, offs):
+        for a, b in offs:
+            pl.semaphore_signal(sem, inc=1, device_id=peer(a, b), device_id_type=MESH)
+
     barrier = pltpu.get_barrier_semaphore()
-    for a, b in peers:
-        pl.semaphore_signal(barrier, inc=1, device_id=peer(a, b), device_id_type=MESH)
+    near = ring(1, True, True)
+    rounds, radius = [], 1
+    while radius < max(nlat // 2, nlon // 2):
+        rounds.append(ring(radius, radius < nlat // 2, radius < nlon // 2))
+        radius *= 2
+    greet(barrier, near)
 
     loaded(0, fields)
     loaded(1, mk_ref)
@@ -122,7 +133,9 @@
             tile = roll(tile, pos if first else pos + HC, 1)
             buf = jnp.where((lane >= pos) & (lane < pos + HC), tile, buf)
         ref[...] = buf
-    pl.semaphore_wait(barrier, len(peers))
+    pl.semaphore_wait(barrier, len(near))
+    if rounds:
+        greet(hello.at[0], rounds[0])
 
     waits = []
 
@@ -134,16 +147,25 @@
         waits.append(pltpu.make_async_remote_copy(src_ref=whole, dst_ref=whole, send_sem=ssem.at[i],
                                                   recv_sem=rsem.at[i], device_id=peer(0, 1), device_id_type=MESH))
 
-    lo, hi = pl.ds(0, HR), pl.ds(rows - HR, HR)
+    lo, hi, lo2, hi2 = (pl.ds(i, HB) for i in (0, rows - HB, HB, rows - 2 * HB))
     send(row_n, [(fields.at[:, lo], row_n, peer(-1, 0))])
     send(row_s, [(fields.at[:, hi], row_s, peer(1, 0))])
     send(mrow_n, [(mk_ref.at[lo], mrow_n, peer(-1, 0))])
     send(mrow_s, [(mk_ref.at[hi], mrow_s, peer(1, 0))])
-    for src, dst, d in ((send_w, recv_e, -1), (send_e, recv_w, 1)):
-        send(dst, [(src.at[lo], dst.at[pl.ds(rows, HR)], peer(-1, d)),
-                   (src.at[hi], dst.at[pl.ds(rows + HR, HR)], peer(1, d)),
+    sides = ((send_w, recv_e, far_e, -1), (send_e, recv_w, far_w, 1))
+    for src, dst, far, d in sides:
+        send(dst, [(src.at[lo], dst.at[pl.ds(rows, HB)], peer(-1, d)),
+                   (src.at[hi], dst.at[pl.ds(rows + HB, HB)], peer(1, d)),
                    (src, dst.at[pl.ds(0, rows)], peer(0, d))])
     early = len(waits)
+    send(far_n, [(fields.at[:, lo2], far_n, peer(-1, 0))])
+    send(far_s, [(fields.at[:, hi2], far_s, peer(1, 0))])
+    send(mfar_n, [(mk_ref.at[lo2], mfar_n, peer(-1, 0))])
+    send(mfar_s, [(mk_ref.at[hi2], mfar_s, peer(1, 0))])
+    for src, dst, far, d in sides:
+        send(far, [(src.at[lo2], far.at[pl.ds(0, HB)], peer(-1, d)),
+                   (src.at[hi2], far.at[pl.ds(HB, HB)], peer(1, d))])
+    late = len(waits)
     loaded(2, w_ref)
     send(wrow_n, [(w_ref.at[pl.ds(0, HW)], wrow_n, peer(-1, 0))])
     send(wrow_s, [(w_ref.at[pl.ds(rows - HS, HS)], wrow_s, peer(1, 0))])
@@ -163,40 +185,48 @@
         send(dst, [(src, dst.at[pl.ds(0, strips)], peer(0, d)),
                    (src.at[pl.ds(0, 1)], dst.at[pl.ds(strips, 1)], peer(-1, d)),
                    (src.at[pl.ds(strips - 1, 1)], dst.at[pl.ds(strips + 1, 1)], peer(1, d))])
+    for i in range(1, len(rounds)):
+        pl.semaphore_wait(hello.at[i - 1], len(rounds[i - 1]))
+        greet(hello.at[i], rounds[i])
     for c in waits[:early]:
         c.wait_recv()
 
-    full = rows + 2 * HR
-    lane = lax.broadcasted_iota(jnp.int32, (full, 128), 1)
-    got_e, got_w = recv_e[...], recv_w[...]
-
-    def side(pos, width):
-        a = roll(got_e, -pos, 1)
-        b = roll(got_w, 128 - width - pos, 1)
-        return jnp.where(lane < width, a, jnp.where(lane >= 128 - width, b, 0.0))
-
-    def padded(i):
-        if i < 4:
-            top, mid, low = row_n[i], wide[i][...], row_s[i]
-        else:
-            top, mid, low = (r[...].astype(jnp.float32) for r in (mrow_n, mk_ref, mrow_s))
-        return jnp.concatenate([jnp.concatenate([mid, top, low], axis=0), side(HC * i, HC)], axis=1)
-
-    ringc = cols + 128
-    row_id = lax.broadcasted_iota(jnp.int32, (full, ringc), 0)
+    full = rows + 2 * HB
     keep_n = (lat < nlat - 1).astype(jnp.float32)
     keep_s = (lat > 0).astype(jnp.float32)
-    edge = jnp.where(row_id < rows, 1.0, jnp.where(row_id < rows + HR, keep_n, keep_s))
-    wet = padded(4) * edge
-    ex = padded(1) * wet * east(wet)
-    ey = padded(2) * wet * north(wet)
-    base = wet * padded(3) + 1.0 - wet
-    diag = base + ex + roll(ex, 1, 1) + ey + roll(ey, 1, 0)
-    rs = lax.rsqrt(diag)
-    rs = rs * (1.5 - 0.5 * diag * rs * rs)
-    rs_e, rs_n = rs * east(rs), rs * north(rs)
-    e2 = 2.0 * ex * rs_e
-    n2 = 2.0 * ey * rs_n
+
+    def operator(mains, got_e, got_w, runs):
+        height = got_e.shape[0]
+        lane = lax.broadcasted_iota(jnp.int32, (height, 128), 1)
+
+        def padded(i):
+            a = roll(got_e, -HC * i, 1)
+            b = roll(got_w, 128 - HC - HC * i, 1)
+            side = jnp.where(lane < HC, a, jnp.where(lane >= 128 - HC, b, 0.0))
+            return jnp.concatenate([mains(i), side], axis=1)
+
+        edge = jnp.concatenate([jnp.full((n, cols + 128), k, jnp.float32) for n, k in runs], axis=0)
+        wet = padded(4) * edge
+        ex = padded(1) * wet * east(wet)
+        ey = padded(2) * wet * north(wet)
+        base = wet * padded(3) + 1.0 - wet
+        diag = base + ex + roll(ex, 1, 1) + ey + roll(ey, 1, 0)
+        rs = lax.rsqrt(diag)
+        rs = rs * (1.5 - 0.5 * diag * rs * rs)
+        rs_e, rs_n = rs * east(rs), rs * north(rs)
+        return wet, rs, rs_e, rs_n, 2.0 * ex * rs_e, 2.0 * ey * rs_n, rs * padded(0)
+
+    def stacked(order):
+        def mains(i):
+            if i < 4:
+                return jnp.concatenate([ref[i] if at is None else ref[i, at] for ref, _, at in order], axis=0)
+            return jnp.concatenate([(ref[...] if at is None else ref[at]) for _, ref, at in order],
+                                   axis=0).astype(jnp.float32)
+        return mains
+
+    wet, rs, rs_e, rs_n, e2, n2, u0 = operator(
+        stacked(((fields, mk_ref, None), (row_n, mrow_n, None), (row_s, mrow_s, None))),
+        recv_e[...], recv_w[...], ((rows, 1.0), (HB, keep_n), (HB, keep_s)))
     e2r[...], n2r[...], rsr[...] = e2, n2, rs
     rz = rows + HB
 
@@ -214,14 +244,13 @@
         s = e2 * le + roll(e2 * prev, 1, 1) + n2 * ln + roll(n2 * prev, 1, 0)
         return s if k == 1 else s - (prev2 + prev2 if k == 2 else prev2)
 
-    us = [rs * padded(0)]
+    us = [u0]
     for k in range(1, ITERS + 1):
         le, ln = east(us[k - 1]), north(us[k - 1])
         keep(k - 1, us[k - 1])
         ue[k - 1], unn[k - 1] = le[:rows, :cols], ln[:rows, :cols]
         us.append(step(k, None, us[k - 1], us[k - 2] if k > 1 else None, le, ln, e2, n2))
     keep(ITERS, us[ITERS])
-    up[(ITERS - 1) % 2], up[ITERS % 2] = us[ITERS - 1], us[ITERS]
 
     inner = [u[:rows, :cols] for u in us]
     rs_in = rs[:rows, :cols]
@@ -266,13 +295,38 @@
         return parts[0]
 
     first_reduce = len(waits)
+    if rounds:
+        pl.semaphore_wait(hello.at[len(rounds) - 1], len(rounds[-1]))
     group = start(0, mine)
 
+    for c in waits[early:late]:
+        c.wait_recv()
+
+    def band_of(near, far):
+        return jnp.concatenate([near[rows - HB:rows], near[rows:rows + HB], far[...],
+                                near[rows + HB:], near[:HB]], axis=0)
+
+    low, high = slice(rows - HB, rows), slice(0, HB)
+    _, _, _, _, e2b, n2b, b0 = operator(
+        stacked(((fields, mk_ref, low), (row_n, mrow_n, None), (far_n, mfar_n, None),
+                 (far_s, mfar_s, None), (row_s, mrow_s, None), (fields, mk_ref, high))),
+        band_of(recv_e, far_e), band_of(recv_w, far_w),
+        ((HB, 1.0), (2 * HB, keep_n), (2 * HB, keep_s), (HB, 1.0)))
+    band = [b0]
+    for k in range(1, ITERS + 1):
+        band.append(step(k, None, band[-1], band[-2] if k > 1 else None, east(band[-1]), north(band[-1]), e2b, n2b))
+
+    def joined(main, halo):
+        return jnp.concatenate([main[:rows], halo[HB:5 * HB]], axis=0)
+
+    e2w[...], n2w[...] = joined(e2, e2b), joined(n2, n2b)
+    for k in (ITERS - 1, ITERS):
+        up[k % 2] = joined(us[k], band[k])
     for k in range(ITERS + 1, DEG):
         prev, prev2 = up[(k - 1) % 2], up[k % 2]
         le, ln = east(prev), north(prev)
         ue[k - 1], unn[k - 1] = le[:rows, :cols], ln[:rows, :cols]
-        x = step(k, None, prev, prev2, le, ln, e2r[...], n2r[...])
+        x = step(k, None, prev, prev2, le, ln, e2w[...], n2w[...])
         keep(k, x)
         up[k % 2] = x
 
@@ -317,7 +371,7 @@
     lax.fori_loop(0, rz // 8, products, 0)
     lax.fori_loop(0, rows // 8, cross, 0)
 
-    for c in waits[early:first_reduce]:
+    for c in waits[late:first_reduce]:
         c.wait_recv()
 
     for j in range(strips + 2):
@@ -502,7 +556,7 @@
 
     def body(forcing, depth_east, depth_north, surface_term, ocean_mask, cost_weights):
         costs, rows, cols = cost_weights.shape
-        full, ringc = rows + 2 * HR, cols + 128
+        full, ringc = rows + 2 * HB, cols + 128
         f32 = jnp.float32
         dma = pltpu.SemaphoreType.DMA
         every = [(a, b) for a in range(nlat) for b in range(nlon) if a or b]
@@ -532,22 +586,22 @@
                 dma((3,)),
                 pltpu.VMEM((rows, 128), f32),
                 pltpu.VMEM((rows, 128), f32),
-                pltpu.VMEM((full, 128), f32),
-                pltpu.VMEM((full, 128), f32),
-                pltpu.VMEM((4, HR, cols), f32),
-                pltpu.VMEM((4, HR, cols), f32),
-                pltpu.VMEM((HR, cols), jnp.int32),
-                pltpu.VMEM((HR, cols), jnp.int32),
+                *[pltpu.VMEM((full, 128), f32)] * 2,
+                *[pltpu.VMEM((2 * HB, 128), f32)] * 2,
+                *[pltpu.VMEM((4, HB, cols), f32)] * 4,
+                *[pltpu.VMEM((HB, cols), jnp.int32)] * 4,
                 pltpu.VMEM((HW, costs, cols), f32),
                 pltpu.VMEM((HS, costs, cols), f32),
                 *[pltpu.VMEM((rows // 8, costs, 128), f32)] * 2,
                 *[pltpu.VMEM((rows // 8 + 2, costs, 128), f32)] * 2,
-                pltpu.VMEM((2, full, ringc), f32),
+                pltpu.VMEM((2, rows + 4 * HB, ringc), f32),
                 pltpu.VMEM((DEG - 1, rows, cols), f32),
                 *[pltpu.VMEM((full, ringc), f32)] * 3,
+                *[pltpu.VMEM((rows + 4 * HB, ringc), f32)] * 2,
                 pltpu.VMEM((rows // 8 + 2, costs, 128), f32),
-                dma((10,)),
-                dma((10,)),
+                dma((16,)),
+                dma((16,)),
+                pltpu.SemaphoreType.REGULAR((max(1, (max(nlat, nlon) - 1).bit_length() - 1),)),
                 *reduce_scratch,
             ],
             compiler_params=pltpu.CompilerParams(

time: 25.4 us -> 23.8 us (0.937)
  Pallas kernels: 24.6 us -> 23 us
    pallas_call x1, Pallas kernels: 19.6 us -> 18 us  [body(): pl.pallas_call(functools.partial(kernel, nlat, nlon, stages), out_shape=[...]
where the time goes in v2:
time: 23.8 us; the launch traced here: 23.6 us
  Pallas kernels  23 us (97%)
  between operations  0.64 us (3%)
    pallas_call x1, Pallas kernels, body(): pl.pallas_call(functools.partial(kernel, nlat, nlon, stages), out_shape=[...  18 us
    pallas_call x1, Pallas kernels, body(): pl.pallas_call(adjoint_kernel, out_shape=[jax.ShapeDtypeStruct(out, f32)]...  5.03 us

profile of v2, /device:TPU:0, one launch (start us, length us, event | category | flops | bytes accessed | tf_op | source)
XLA Modules:
  0.0 23.6 jit_solution(15836152298224045614)
XLA Ops:
  0.6 18.0 %shard_map.85 = (f32[12,72,256]{2,1,0:T(8,128)S(1)}, f32[11,64,256]{2,1,0:T(8,128)S(1)}, f32[11,64,256]{2,1,0:T(8,128)S(1)}, f32[11,64,256]{2,1,0:T(8,128)S(1)},...) custom-call(f32[64,256]{1,0:T(8,128)} %f_hbm.1, ...), custom_call_target="tpu_custom_call" | custom-call | tf_op jit(solution)/shard_map/pallas_call | solution.py:577
  18.6 5.0 %shard_map.86 = (f32[8,64,256]{2,1,0:T(8,128)}, f32[8,64,256]{2,1,0:T(8,128)}, f32[8,64,256]{2,1,0:T(8,128)}) custom-call(f32[12,72,256]{2,1,0:T(8,128)S(1)} %get-tuple-element.15.un, f32[11,64,256]{2,1,0:T(8,128)S(1)} %get-tuple-element.16.ue, f32[11,64,256]{2,1,0:T(8,128)S(1)} %get-tuple-element.17.xe, f32[11,64,256]{2,1,0:T(8,128)S(1)} %get-tuple-element.18.xn, ...), custom_call_target="tpu_custom_call" | custom-call | tf_op jit(solution)/shard_map/pallas_call | solution.py:612

commit v3 on v2

--- a/solution.py
+++ b/solution.py
@@ -12,6 +12,7 @@
 HB = 8
 HS = 5
 BLOCK = 8
+GROUPED = 4
 HC = 13
 HW = 6
 GROUP = 16
@@ -85,9 +86,9 @@
 def kernel(nlat, nlon, stages, f_hbm, de_hbm, dn_hbm, st_hbm, mk_hbm, w_hbm,
            un, ue, xe, xn, ww, v, ve, geo, dia, coef, us_side, vs_side,
            fields, mk_ref, w_ref, lsem,
-           send_w, send_e, recv_e, recv_w, far_e, far_w, row_n, row_s, far_n, far_s,
-           mrow_n, mrow_s, mfar_n, mfar_s, wrow_n, wrow_s,
-           wsend_w, wsend_e, wrecv_e, wrecv_w, up, unn, e2r, n2r, rsr, e2w, n2w, comb, ssem, rsem, hello,
+           send_w, send_e, main, row_n, row_s, cor_n, cor_s, far_n, far_s, farc_n, farc_s,
+           wrow_n, wrow_s, wsend_w, wsend_e, wmain, wcor_n, wcor_s,
+           up, unn, e2r, n2r, rsr, e2w, n2w, comb, ssem, rsem, hello,
            *reduce_refs):
     lat, lon = lax.axis_index("lat"), lax.axis_index("lon")
     rows, costs, cols = w_ref.shape
@@ -103,72 +104,123 @@
     def peer(dlat, dlon):
         return (lax.rem(lat + dlat + nlat, nlat), lax.rem(lon + dlon + nlon, nlon))
 
-    def ring(radius, lat_too, lon_too):
-        offs = {(a % nlat, b % nlon) for a in ((-radius, 0, radius) if lat_too else (0,))
-                for b in ((-radius, 0, radius) if lon_too else (0,))}
-        return sorted(offs - {(0, 0)})
-
-    def greet(sem, offs):
-        for a, b in offs:
-            pl.semaphore_signal(sem, inc=1, device_id=peer(a, b), device_id_type=MESH)
+    has_s, has_n = lat > 0, lat < nlat - 1
+
+    def beside(r):
+        return sorted({-r % nlon, 0, r % nlon})
+
+    def greet(sem, r):
+        for dlat, there in ((0, None), (-r, lat >= r), (r, lat < nlat - r)):
+            def go(dlat=dlat):
+                for b in beside(r):
+                    if dlat or b:
+                        pl.semaphore_signal(sem, inc=1, device_id=(lat + dlat, lax.rem(lon + b, nlon)),
+                                            device_id_type=MESH)
+            if there is None:
+                go()
+            elif r < nlat:
+                pl.when(there)(go)
+
+    def greeted(sem, r):
+        lines = 1 + (lat >= r).astype(jnp.int32) + (lat < nlat - r).astype(jnp.int32)
+        pl.semaphore_wait(sem, lines * len(beside(r)) - 1)
 
     barrier = pltpu.get_barrier_semaphore()
-    near = ring(1, True, True)
     rounds, radius = [], 1
-    while radius < max(nlat // 2, nlon // 2):
-        rounds.append(ring(radius, radius < nlat // 2, radius < nlon // 2))
+    while radius < max(nlat - 1, nlon // 2):
+        rounds.append(radius)
         radius *= 2
-    greet(barrier, near)
-
-    loaded(0, fields)
+    greet(barrier, 1)
+
+    @pl.when(lat == nlat - 1)
+    def _():
+        for ref in (row_n, cor_n, far_n, farc_n, wrow_n, wcor_n):
+            ref[...] = jnp.zeros_like(ref)
+
+    @pl.when(lat == 0)
+    def _():
+        for ref in (row_s, cor_s, far_s, farc_s, wrow_s, wcor_s):
+            ref[...] = jnp.zeros_like(ref)
+
+    loaded(0, fields.at[pl.ds(0, 4)])
     loaded(1, mk_ref)
+    fields[4] = mk_ref[...].astype(jnp.float32)
 
     lane = lax.broadcasted_iota(jnp.int32, (rows, 128), 1)
-    wide = [fields.at[i] for i in range(4)] + [mk_ref]
     for ref, at, first in ((send_w, slice(0, 128), True), (send_e, slice(cols - 128, cols), False)):
         buf = jnp.zeros((rows, 128), jnp.float32)
         for i in range(5):
             pos = HC * i
-            tile = wide[i][:, at].astype(jnp.float32)
+            tile = fields[i, :, at]
             tile = roll(tile, pos if first else pos + HC, 1)
             buf = jnp.where((lane >= pos) & (lane < pos + HC), tile, buf)
         ref[...] = buf
-    pl.semaphore_wait(barrier, len(near))
+    greeted(barrier, 1)
     if rounds:
         greet(hello.at[0], rounds[0])
 
-    waits = []
-
-    def send(whole, parts):
-        i = len(waits)
-        for src, dst, dev in parts:
-            pltpu.make_async_remote_copy(src_ref=src, dst_ref=dst, send_sem=ssem.at[i], recv_sem=rsem.at[i],
-                                         device_id=dev, device_id_type=MESH).start()
-        waits.append(pltpu.make_async_remote_copy(src_ref=whole, dst_ref=whole, send_sem=ssem.at[i],
-                                                  recv_sem=rsem.at[i], device_id=peer(0, 1), device_id_type=MESH))
+    groups, pending = [], []
+
+    def whole(i):
+        ref = groups[i][0]
+        return pltpu.make_async_remote_copy(src_ref=ref, dst_ref=ref, send_sem=ssem.at[i], recv_sem=rsem.at[i],
+                                            device_id=peer(0, 1), device_id_type=MESH)
+
+    def send(ref, side, parts):
+        i = len(groups)
+        groups.append((ref, side))
+        pending.append((i, side, parts))
+
+    def depart():
+        for i, side, parts in pending:
+            def go(i=i, parts=parts):
+                for src, dst, dev in parts:
+                    pltpu.make_async_remote_copy(src_ref=src, dst_ref=dst, send_sem=ssem.at[i], recv_sem=rsem.at[i],
+                                                 device_id=dev, device_id_type=MESH).start()
+            if side == 0:
+                go()
+            else:
+                pl.when(has_s if side > 0 else has_n)(go)
+        pending.clear()
+
+    def arrive(span):
+        for i in span:
+            side = groups[i][1]
+            if side == 0:
+                whole(i).wait_recv()
+            else:
+                pl.when(has_n if side > 0 else has_s)(lambda i=i: whole(i).wait_recv())
+
+    def sent(span):
+        for i in span:
+            side = groups[i][1]
+            if side == 0:
+                whole(i).wait_send()
+            else:
+                pl.when(has_s if side > 0 else has_n)(lambda i=i: whole(i).wait_send())
 
     lo, hi, lo2, hi2 = (pl.ds(i, HB) for i in (0, rows - HB, HB, rows - 2 * HB))
-    send(row_n, [(fields.at[:, lo], row_n, peer(-1, 0))])
-    send(row_s, [(fields.at[:, hi], row_s, peer(1, 0))])
-    send(mrow_n, [(mk_ref.at[lo], mrow_n, peer(-1, 0))])
-    send(mrow_s, [(mk_ref.at[hi], mrow_s, peer(1, 0))])
-    sides = ((send_w, recv_e, far_e, -1), (send_e, recv_w, far_w, 1))
-    for src, dst, far, d in sides:
-        send(dst, [(src.at[lo], dst.at[pl.ds(rows, HB)], peer(-1, d)),
-                   (src.at[hi], dst.at[pl.ds(rows + HB, HB)], peer(1, d)),
-                   (src, dst.at[pl.ds(0, rows)], peer(0, d))])
-    early = len(waits)
-    send(far_n, [(fields.at[:, lo2], far_n, peer(-1, 0))])
-    send(far_s, [(fields.at[:, hi2], far_s, peer(1, 0))])
-    send(mfar_n, [(mk_ref.at[lo2], mfar_n, peer(-1, 0))])
-    send(mfar_s, [(mk_ref.at[hi2], mfar_s, peer(1, 0))])
-    for src, dst, far, d in sides:
-        send(far, [(src.at[lo2], far.at[pl.ds(0, HB)], peer(-1, d)),
-                   (src.at[hi2], far.at[pl.ds(HB, HB)], peer(1, d))])
-    late = len(waits)
+
+    def corners(to, side, at):
+        send(to, side, [(send_w.at[at], to.at[0], peer(-side, -1)), (send_e.at[at], to.at[1], peer(-side, 1))])
+
+    corners(cor_n, 1, lo)
+    corners(cor_s, -1, hi)
+    send(row_n, 1, [(fields.at[:, lo], row_n, peer(-1, 0))])
+    send(row_s, -1, [(fields.at[:, hi], row_s, peer(1, 0))])
+    send(main, 0, [(send_w, main.at[0], peer(0, -1)), (send_e, main.at[1], peer(0, 1))])
+    depart()
+    early = len(groups)
+    corners(farc_n, 1, lo2)
+    corners(farc_s, -1, hi2)
+    send(far_n, 1, [(fields.at[:, lo2], far_n, peer(-1, 0))])
+    send(far_s, -1, [(fields.at[:, hi2], far_s, peer(1, 0))])
+    depart()
+    late = len(groups)
     loaded(2, w_ref)
-    send(wrow_n, [(w_ref.at[pl.ds(0, HW)], wrow_n, peer(-1, 0))])
-    send(wrow_s, [(w_ref.at[pl.ds(rows - HS, HS)], wrow_s, peer(1, 0))])
+    send(wrow_n, 1, [(w_ref.at[pl.ds(0, HW)], wrow_n, peer(-1, 0))])
+    send(wrow_s, -1, [(w_ref.at[pl.ds(rows - HS, HS)], wrow_s, peer(1, 0))])
+    depart()
     lane8 = lax.broadcasted_iota(jnp.int32, (costs, 128), 1)
     sub8 = lax.broadcasted_iota(jnp.int32, (costs, 128), 0)
     for j in range(rows // 8):
@@ -181,21 +233,17 @@
             to_e = jnp.where((lane8 >= end - HS) & (lane8 < end), roll(last, at, 1), to_e)
         wsend_w[j], wsend_e[j] = to_w, to_e
     strips = rows // 8
-    for src, dst, d in ((wsend_w, wrecv_e, -1), (wsend_e, wrecv_w, 1)):
-        send(dst, [(src, dst.at[pl.ds(0, strips)], peer(0, d)),
-                   (src.at[pl.ds(0, 1)], dst.at[pl.ds(strips, 1)], peer(-1, d)),
-                   (src.at[pl.ds(strips - 1, 1)], dst.at[pl.ds(strips + 1, 1)], peer(1, d))])
+    for to, side, j in ((wcor_n, 1, 0), (wcor_s, -1, strips - 1)):
+        send(to, side, [(wsend_w.at[j], to.at[0], peer(-side, -1)), (wsend_e.at[j], to.at[1], peer(-side, 1))])
+    send(wmain, 0, [(wsend_w, wmain.at[0], peer(0, -1)), (wsend_e, wmain.at[1], peer(0, 1))])
+    depart()
     for i in range(1, len(rounds)):
-        pl.semaphore_wait(hello.at[i - 1], len(rounds[i - 1]))
+        greeted(hello.at[i - 1], rounds[i - 1])
         greet(hello.at[i], rounds[i])
-    for c in waits[:early]:
-        c.wait_recv()
+    arrive(range(early))
 
     full = rows + 2 * HB
-    keep_n = (lat < nlat - 1).astype(jnp.float32)
-    keep_s = (lat > 0).astype(jnp.float32)
-
-    def operator(mains, got_e, got_w, runs):
+    def operator(mains, got_e, got_w):
         height = got_e.shape[0]
         lane = lax.broadcasted_iota(jnp.int32, (height, 128), 1)
 
@@ -205,8 +253,7 @@
             side = jnp.where(lane < HC, a, jnp.where(lane >= 128 - HC, b, 0.0))
             return jnp.concatenate([mains(i), side], axis=1)
 
-        edge = jnp.concatenate([jnp.full((n, cols + 128), k, jnp.float32) for n, k in runs], axis=0)
-        wet = padded(4) * edge
+        wet = padded(4)
         ex = padded(1) * wet * east(wet)
         ey = padded(2) * wet * north(wet)
         base = wet * padded(3) + 1.0 - wet
@@ -217,16 +264,13 @@
         return wet, rs, rs_e, rs_n, 2.0 * ex * rs_e, 2.0 * ey * rs_n, rs * padded(0)
 
     def stacked(order):
-        def mains(i):
-            if i < 4:
-                return jnp.concatenate([ref[i] if at is None else ref[i, at] for ref, _, at in order], axis=0)
-            return jnp.concatenate([(ref[...] if at is None else ref[at]) for _, ref, at in order],
-                                   axis=0).astype(jnp.float32)
-        return mains
+        return lambda i: jnp.concatenate([ref[i] if at is None else ref[i, at] for ref, at in order], axis=0)
+
+    def strip(j):
+        return jnp.concatenate([main[j], cor_n[j], cor_s[j]], axis=0)
 
     wet, rs, rs_e, rs_n, e2, n2, u0 = operator(
-        stacked(((fields, mk_ref, None), (row_n, mrow_n, None), (row_s, mrow_s, None))),
-        recv_e[...], recv_w[...], ((rows, 1.0), (HB, keep_n), (HB, keep_s)))
+        stacked(((fields, None), (row_n, None), (row_s, None))), strip(0), strip(1))
     e2r[...], n2r[...], rsr[...] = e2, n2, rs
     rz = rows + HB
 
@@ -294,24 +338,21 @@
             parts = [sum(parts[i:i + 2][1:], parts[i]) for i in range(0, len(parts), 2)]
         return parts[0]
 
-    first_reduce = len(waits)
+    waits = []
     if rounds:
-        pl.semaphore_wait(hello.at[len(rounds) - 1], len(rounds[-1]))
+        greeted(hello.at[len(rounds) - 1], rounds[-1])
     group = start(0, mine)
 
-    for c in waits[early:late]:
-        c.wait_recv()
-
-    def band_of(near, far):
-        return jnp.concatenate([near[rows - HB:rows], near[rows:rows + HB], far[...],
-                                near[rows + HB:], near[:HB]], axis=0)
+    arrive(range(early, late))
 
     low, high = slice(rows - HB, rows), slice(0, HB)
+
+    def strip_band(j):
+        return jnp.concatenate([main[j, low], cor_n[j], farc_n[j], farc_s[j], cor_s[j], main[j, high]], axis=0)
+
     _, _, _, _, e2b, n2b, b0 = operator(
-        stacked(((fields, mk_ref, low), (row_n, mrow_n, None), (far_n, mfar_n, None),
-                 (far_s, mfar_s, None), (row_s, mrow_s, None), (fields, mk_ref, high))),
-        band_of(recv_e, far_e), band_of(recv_w, far_w),
-        ((HB, 1.0), (2 * HB, keep_n), (2 * HB, keep_s), (HB, 1.0)))
+        stacked(((fields, low), (row_n, None), (far_n, None), (far_s, None), (row_s, None), (fields, high))),
+        strip_band(0), strip_band(1))
     band = [b0]
     for k in range(1, ITERS + 1):
         band.append(step(k, None, band[-1], band[-2] if k > 1 else None, east(band[-1]), north(band[-1]), e2b, n2b))
@@ -371,11 +412,12 @@
     lax.fori_loop(0, rz // 8, products, 0)
     lax.fori_loop(0, rows // 8, cross, 0)
 
-    for c in waits[late:first_reduce]:
-        c.wait_recv()
+    arrive(range(late, len(groups)))
 
     for j in range(strips + 2):
-        comb[j] = jnp.where(lane8 % GROUP < HW, wrecv_e[j], wrecv_w[j])
+        a, b = ((wmain.at[0, j], wmain.at[1, j]) if j < strips else
+                (wcor_n.at[0], wcor_n.at[1]) if j == strips else (wcor_s.at[0], wcor_s.at[1]))
+        comb[j] = jnp.where(lane8 % GROUP < HW, a[...], b[...])
 
     def ring_row(r):
         return r if r >= 0 else full + r
@@ -442,6 +484,7 @@
     for s in range(DEG):
         coef[CH + s] = tail[s] + tail[s + 2] if s else 2.0 * tail[0]
         coef[CM + s] = bar[s] if s else 2.0 * bar[0]
+    sent(range(len(groups)))
     for c in waits:
         c.wait_send()
 
@@ -501,42 +544,42 @@
             acc = acc + factor(CH + s, cols) * line(ww, s, r)
         return acc * line(dia, r)
 
-    def row(r, above):
-        ge = gn = fa = db = None
-
+    def rows_of(rs, above):
         def add(acc, term):
             return term if acc is None else acc + term
 
-        for a in range(ITERS):
-            x = v[a, r + HS, :, :cols]
-            db = add(db, x * line(z, a, r))
-            fa = add(fa, x * factor(CC + a, cols))
-            if a < ITERS - 1:
-                here = line(y, a, r)
-                ge = add(ge, x * line(ye, a, r) + ve[a, r] * here)
-                gn = add(gn, x * line(y, a, r + 1) + v[a, r + HS + 1, :, :cols] * here)
-        for s in range(DEG):
-            db = add(db, factor(CH + s, cols) * line(ww, s, r))
-            fa = add(fa, factor(CM + s, cols) * line(un, s, r))
-            if s < DEG - 1:
-                c = factor(CX + s, cols)
-                ge = add(ge, c * line(xe, s, r))
-                gn = add(gn, c * line(xn, s, r))
-        db = db * line(dia, r)
-        end = jnp.concatenate([pltpu.roll(side, 127 - r, 1)] * (cols // 128), axis=1)
-        db_e = jnp.where(lane_c == cols - 1, end, east(db))
-        fa_ref[r] = line(geo, 4, r) * fa
-        ge_ref[r] = line(geo, 2, r) * ge + line(geo, 0, r) * (db + db_e)
-        gn_ref[r] = line(geo, 3, r) * gn + line(geo, 1, r) * (db + above)
-        return db
+        ge, gn, fa, db = ([None] * len(rs) for _ in range(4))
+        for i, r in enumerate(rs):
+            for a in range(ITERS):
+                x = v[a, r + HS, :, :cols]
+                db[i] = add(db[i], x * line(z, a, r))
+                fa[i] = add(fa[i], x * factor(CC + a, cols))
+                if a < ITERS - 1:
+                    here = line(y, a, r)
+                    ge[i] = add(ge[i], x * line(ye, a, r) + ve[a, r] * here)
+                    gn[i] = add(gn[i], x * line(y, a, r + 1) + v[a, r + HS + 1, :, :cols] * here)
+        for first, count, acc, field in ((CH, DEG, db, ww), (CX, DEG - 1, ge, xe), (CX, DEG - 1, gn, xn), (CM, DEG, fa, un)):
+            for s in range(count):
+                c = factor(first + s, cols)
+                for i, r in enumerate(rs):
+                    acc[i] = acc[i] + c * line(field, s, r)
+        for i, r in enumerate(rs):
+            d = db[i] * line(dia, r)
+            end = jnp.concatenate([pltpu.roll(side, 127 - r, 1)] * (cols // 128), axis=1)
+            d_e = jnp.where(lane_c == cols - 1, end, east(d))
+            fa_ref[r] = line(geo, 4, r) * fa[i]
+            ge_ref[r] = line(geo, 2, r) * ge[i] + line(geo, 0, r) * (d + d_e)
+            gn_ref[r] = line(geo, 3, r) * gn[i] + line(geo, 1, r) * (d + above)
+            above = d
+        return above
 
     parts = 2
     size = rows // parts
 
     def block(i, above):
         first = rows - (i + 1) * BLOCK
-        for j in range(BLOCK - 1, -1, -1):
-            above = row(first + j, above)
+        for j in range(BLOCK - 1, -1, -GROUPED):
+            above = rows_of([first + j - i for i in range(GROUPED)], above)
         return above
 
     above = diag_of(rows)
@@ -580,28 +623,30 @@
             in_specs=[hbm] * 6,
             out_specs=[vmem] * len(shapes),
             scratch_shapes=[
-                pltpu.VMEM((4, rows, cols), f32),
+                pltpu.VMEM((5, rows, cols), f32),
                 pltpu.VMEM((rows, cols), jnp.int32),
                 pltpu.VMEM((rows, costs, cols), f32),
                 dma((3,)),
                 pltpu.VMEM((rows, 128), f32),
                 pltpu.VMEM((rows, 128), f32),
-                *[pltpu.VMEM((full, 128), f32)] * 2,
-                *[pltpu.VMEM((2 * HB, 128), f32)] * 2,
-                *[pltpu.VMEM((4, HB, cols), f32)] * 4,
-                *[pltpu.VMEM((HB, cols), jnp.int32)] * 4,
+                pltpu.VMEM((2, rows, 128), f32),
+                *[pltpu.VMEM((5, HB, cols), f32)] * 2,
+                *[pltpu.VMEM((2, HB, 128), f32)] * 2,
+                *[pltpu.VMEM((5, HB, cols), f32)] * 2,
+                *[pltpu.VMEM((2, HB, 128), f32)] * 2,
                 pltpu.VMEM((HW, costs, cols), f32),
                 pltpu.VMEM((HS, costs, cols), f32),
                 *[pltpu.VMEM((rows // 8, costs, 128), f32)] * 2,
-                *[pltpu.VMEM((rows // 8 + 2, costs, 128), f32)] * 2,
+                pltpu.VMEM((2, rows // 8, costs, 128), f32),
+                *[pltpu.VMEM((2, costs, 128), f32)] * 2,
                 pltpu.VMEM((2, rows + 4 * HB, ringc), f32),
                 pltpu.VMEM((DEG - 1, rows, cols), f32),
                 *[pltpu.VMEM((full, ringc), f32)] * 3,
                 *[pltpu.VMEM((rows + 4 * HB, ringc), f32)] * 2,
                 pltpu.VMEM((rows // 8 + 2, costs, 128), f32),
-                dma((16,)),
-                dma((16,)),
-                pltpu.SemaphoreType.REGULAR((max(1, (max(nlat, nlon) - 1).bit_length() - 1),)),
+                dma((14,)),
+                dma((14,)),
+                pltpu.SemaphoreType.REGULAR((max(1, (max(nlat - 1, nlon // 2) - 1).bit_length()),)),
                 *reduce_scratch,
             ],
             compiler_params=pltpu.CompilerParams(

time: 23.8 us -> 23 us (0.966)
  Pallas kernels: 23 us -> 22.2 us
    pallas_call x1, Pallas kernels: 18 us -> 17.3 us  [body(): pl.pallas_call(functools.partial(kernel, nlat, nlon, stages), out_shape=[...]
where the time goes in v3:
time: 23 us; the launch traced here: 22.9 us
  Pallas kernels  22.2 us (97%)
  between operations  0.64 us (3%)
    pallas_call x1, Pallas kernels, body(): pl.pallas_call(functools.partial(kernel, nlat, nlon, stages), out_shape=[...  17.3 us
    pallas_call x1, Pallas kernels, body(): pl.pallas_call(adjoint_kernel, out_shape=[jax.ShapeDtypeStruct(out, f32)]...  4.92 us

profile of v3, /device:TPU:0, one launch (start us, length us, event | category | flops | bytes accessed | tf_op | source)
XLA Modules:
  0.0 22.9 jit_solution(16040004921863176383)
XLA Ops:
  0.6 17.3 %shard_map.85 = (f32[12,72,256]{2,1,0:T(8,128)S(1)}, f32[11,64,256]{2,1,0:T(8,128)S(1)}, f32[11,64,256]{2,1,0:T(8,128)S(1)}, f32[11,64,256]{2,1,0:T(8,128)S(1)},...) custom-call(f32[64,256]{1,0:T(8,128)} %f_hbm.1, ...), custom_call_target="tpu_custom_call" | custom-call | tf_op jit(solution)/shard_map/pallas_call | solution.py:620
  17.9 4.9 %shard_map.86 = (f32[8,64,256]{2,1,0:T(8,128)}, f32[8,64,256]{2,1,0:T(8,128)}, f32[8,64,256]{2,1,0:T(8,128)}) custom-call(f32[12,72,256]{2,1,0:T(8,128)S(1)} %get-tuple-element.15.un, f32[11,64,256]{2,1,0:T(8,128)S(1)} %get-tuple-element.16.ue, f32[11,64,256]{2,1,0:T(8,128)S(1)} %get-tuple-element.17.xe, f32[11,64,256]{2,1,0:T(8,128)S(1)} %get-tuple-element.18.xn, ...), custom_call_target="tpu_custom_call" | custom-call | tf_op jit(solution)/shard_map/pallas_call | solution.py:657

commit v4 on v3

--- a/solution.py
+++ b/solution.py
@@ -88,7 +88,7 @@
            fields, mk_ref, w_ref, lsem,
            send_w, send_e, main, row_n, row_s, cor_n, cor_s, far_n, far_s, farc_n, farc_s,
            wrow_n, wrow_s, wsend_w, wsend_e, wmain, wcor_n, wcor_s,
-           up, unn, e2r, n2r, rsr, e2w, n2w, comb, ssem, rsem, hello,
+           up, unn, e2r, n2r, rsr, comb, ssem, rsem, hello,
            *reduce_refs):
     lat, lon = lax.axis_index("lat"), lax.axis_index("lon")
     rows, costs, cols = w_ref.shape
@@ -358,16 +358,15 @@
         band.append(step(k, None, band[-1], band[-2] if k > 1 else None, east(band[-1]), north(band[-1]), e2b, n2b))
 
     def joined(main, halo):
-        return jnp.concatenate([main[:rows], halo[HB:5 * HB]], axis=0)
-
-    e2w[...], n2w[...] = joined(e2, e2b), joined(n2, n2b)
+        return jnp.concatenate([main[:rows], halo[HB:2 * HB], halo[4 * HB:5 * HB]], axis=0)
+
     for k in (ITERS - 1, ITERS):
         up[k % 2] = joined(us[k], band[k])
     for k in range(ITERS + 1, DEG):
         prev, prev2 = up[(k - 1) % 2], up[k % 2]
         le, ln = east(prev), north(prev)
         ue[k - 1], unn[k - 1] = le[:rows, :cols], ln[:rows, :cols]
-        x = step(k, None, prev, prev2, le, ln, e2w[...], n2w[...])
+        x = step(k, None, prev, prev2, le, ln, e2r[...], n2r[...])
         keep(k, x)
         up[k % 2] = x
 
@@ -573,8 +572,7 @@
             above = d
         return above
 
-    parts = 2
-    size = rows // parts
+    last = max(BLOCK, rows // 4 // BLOCK * BLOCK)
 
     def block(i, above):
         first = rows - (i + 1) * BLOCK
@@ -583,10 +581,9 @@
         return above
 
     above = diag_of(rows)
-    per = size // BLOCK
-    for p in range(parts):
-        above = lax.fori_loop(p * per, (p + 1) * per, block, above)
-        at = pl.ds(rows - (p + 1) * size, size)
+    for low, high in ((last, rows), (0, last)):
+        above = lax.fori_loop((rows - high) // BLOCK, (rows - low) // BLOCK, block, above)
+        at = pl.ds(low, high - low)
         for i, (src, dst) in enumerate(outs):
             for n in range(costs):
                 pltpu.make_async_copy(src.at[at, n, :], dst.at[n, at], osem.at[i]).start()
@@ -639,10 +636,9 @@
                 *[pltpu.VMEM((rows // 8, costs, 128), f32)] * 2,
                 pltpu.VMEM((2, rows // 8, costs, 128), f32),
                 *[pltpu.VMEM((2, costs, 128), f32)] * 2,
-                pltpu.VMEM((2, rows + 4 * HB, ringc), f32),
+                pltpu.VMEM((2, full, ringc), f32),
                 pltpu.VMEM((DEG - 1, rows, cols), f32),
                 *[pltpu.VMEM((full, ringc), f32)] * 3,
-                *[pltpu.VMEM((rows + 4 * HB, ringc), f32)] * 2,
                 pltpu.VMEM((rows // 8 + 2, costs, 128), f32),
                 dma((14,)),
                 dma((14,)),

time: 23 us -> 22.8 us (level)
  no operation moved by 1% of the time
where the time goes in v4:
time: 22.8 us; the launch traced here: 22.6 us
  Pallas kernels  22 us (96%)
  between operations  0.64 us (3%)
    pallas_call x1, Pallas kernels, body(): pl.pallas_call(functools.partial(kernel, nlat, nlon, stages), out_shape=[...  17.2 us
    pallas_call x1, Pallas kernels, body(): pl.pallas_call(adjoint_kernel, out_shape=[jax.ShapeDtypeStruct(out, f32)]...  4.79 us

profile of v4, /device:TPU:0, one launch (start us, length us, event | category | flops | bytes accessed | tf_op | source)
XLA Modules:
  0.0 22.6 jit_solution(13864512735798091420)
XLA Ops:
  0.6 17.2 %shard_map.85 = (f32[12,72,256]{2,1,0:T(8,128)S(1)}, f32[11,64,256]{2,1,0:T(8,128)S(1)}, f32[11,64,256]{2,1,0:T(8,128)S(1)}, f32[11,64,256]{2,1,0:T(8,128)S(1)},...) custom-call(f32[64,256]{1,0:T(8,128)} %f_hbm.1, ...), custom_call_target="tpu_custom_call" | custom-call | tf_op jit(solution)/shard_map/pallas_call | solution.py:617
  17.8 4.8 %shard_map.86 = (f32[8,64,256]{2,1,0:T(8,128)}, f32[8,64,256]{2,1,0:T(8,128)}, f32[8,64,256]{2,1,0:T(8,128)}) custom-call(f32[12,72,256]{2,1,0:T(8,128)S(1)} %get-tuple-element.15.un, f32[11,64,256]{2,1,0:T(8,128)S(1)} %get-tuple-element.16.ue, f32[11,64,256]{2,1,0:T(8,128)S(1)} %get-tuple-element.17.xe, f32[11,64,256]{2,1,0:T(8,128)S(1)} %get-tuple-element.18.xn, ...), custom_call_target="tpu_custom_call" | custom-call | tf_op jit(solution)/shard_map/pallas_call | solution.py:653

commit v5 on v4

--- a/solution.py
+++ b/solution.py
@@ -163,7 +163,7 @@
 
     def whole(i):
         ref = groups[i][0]
-        return pltpu.make_async_remote_copy(src_ref=ref, dst_ref=ref, send_sem=ssem.at[i], recv_sem=rsem.at[i],
+        return pltpu.make_async_remote_copy(src_ref=ref, dst_ref=ref, send_sem=ssem.at[groups[i][1] % 3], recv_sem=rsem.at[i],
                                             device_id=peer(0, 1), device_id_type=MESH)
 
     def send(ref, side, parts):
@@ -173,9 +173,9 @@
 
     def depart():
         for i, side, parts in pending:
-            def go(i=i, parts=parts):
+            def go(i=i, side=side, parts=parts):
                 for src, dst, dev in parts:
-                    pltpu.make_async_remote_copy(src_ref=src, dst_ref=dst, send_sem=ssem.at[i], recv_sem=rsem.at[i],
+                    pltpu.make_async_remote_copy(src_ref=src, dst_ref=dst, send_sem=ssem.at[side % 3], recv_sem=rsem.at[i],
                                                  device_id=dev, device_id_type=MESH).start()
             if side == 0:
                 go()
@@ -191,13 +191,11 @@
             else:
                 pl.when(has_n if side > 0 else has_s)(lambda i=i: whole(i).wait_recv())
 
-    def sent(span):
-        for i in span:
-            side = groups[i][1]
-            if side == 0:
-                whole(i).wait_send()
-            else:
-                pl.when(has_s if side > 0 else has_n)(lambda i=i: whole(i).wait_send())
+    def sent(side):
+        blocks = sum(ref.size for ref, at in groups if at == side) // (costs * 128)
+        ref = coef.at[pl.ds(0, blocks)]
+        pltpu.make_async_remote_copy(src_ref=ref, dst_ref=ref, send_sem=ssem.at[side % 3], recv_sem=rsem.at[0],
+                                     device_id=peer(0, 1), device_id_type=MESH).wait_send()
 
     lo, hi, lo2, hi2 = (pl.ds(i, HB) for i in (0, rows - HB, HB, rows - 2 * HB))
 
@@ -483,7 +481,9 @@
     for s in range(DEG):
         coef[CH + s] = tail[s] + tail[s + 2] if s else 2.0 * tail[0]
         coef[CM + s] = bar[s] if s else 2.0 * bar[0]
-    sent(range(len(groups)))
+    sent(0)
+    pl.when(has_s)(lambda: sent(1))
+    pl.when(has_n)(lambda: sent(-1))
     for c in waits:
         c.wait_send()
 
@@ -640,7 +640,7 @@
                 pltpu.VMEM((DEG - 1, rows, cols), f32),
                 *[pltpu.VMEM((full, ringc), f32)] * 3,
                 pltpu.VMEM((rows // 8 + 2, costs, 128), f32),
-                dma((14,)),
+                dma((3,)),
                 dma((14,)),
                 pltpu.SemaphoreType.REGULAR((max(1, (max(nlat - 1, nlon // 2) - 1).bit_length()),)),
                 *reduce_scratch,

time: 22.8 us -> 22.7 us (level)
  no operation moved by 1% of the time
where the time goes in v5:
time: 22.7 us; the launch traced here: 22.5 us
  Pallas kernels  21.8 us (96%)
  between operations  0.64 us (3%)
    pallas_call x1, Pallas kernels, body(): pl.pallas_call(functools.partial(kernel, nlat, nlon, stages), out_shape=[...  17.1 us
    pallas_call x1, Pallas kernels, body(): pl.pallas_call(adjoint_kernel, out_shape=[jax.ShapeDtypeStruct(out, f32)]...  4.79 us

profile of v5, /device:TPU:0, one launch (start us, length us, event | category | flops | bytes accessed | tf_op | source)
XLA Modules:
  0.0 22.5 jit_solution(15151401671676856558)
XLA Ops:
  0.6 17.1 %shard_map.85 = (f32[12,72,256]{2,1,0:T(8,128)S(1)}, f32[11,64,256]{2,1,0:T(8,128)S(1)}, f32[11,64,256]{2,1,0:T(8,128)S(1)}, f32[11,64,256]{2,1,0:T(8,128)S(1)},...) custom-call(f32[64,256]{1,0:T(8,128)} %f_hbm.1, ...), custom_call_target="tpu_custom_call" | custom-call | tf_op jit(solution)/shard_map/pallas_call | solution.py:617
  17.7 4.8 %shard_map.86 = (f32[8,64,256]{2,1,0:T(8,128)}, f32[8,64,256]{2,1,0:T(8,128)}, f32[8,64,256]{2,1,0:T(8,128)}) custom-call(f32[12,72,256]{2,1,0:T(8,128)S(1)} %get-tuple-element.15.un, f32[11,64,256]{2,1,0:T(8,128)S(1)} %get-tuple-element.16.ue, f32[11,64,256]{2,1,0:T(8,128)S(1)} %get-tuple-element.17.xe, f32[11,64,256]{2,1,0:T(8,128)S(1)} %get-tuple-element.18.xn, ...), custom_call_target="tpu_custom_call" | custom-call | tf_op jit(solution)/shard_map/pallas_call | solution.py:653
